TPU v7x, 32 devices: a 4x4x1 block of a 4x4x8 slice. The times are simulated.
32 devices in a mesh: dp: 1 (over z), tp: 32 (over y, x, core).
Axes of the slice: x: 4, y: 4, z: 1, core: 2. Of those that a mesh axis runs over, the one named last changes fastest.
The devices are a block of a 4x4x8 slice.
Arguments:
- tokens_in: bfloat16 [32, 256, 4096], P('dp')
- ln_gain: float32 [4096], replicated
- ln_bias: float32 [4096], replicated
- w_qkv: bfloat16 [4096, 32, 384], P(None, 'tp')
- w_out: bfloat16 [4096, 4096], P('tp')
- w_up: bfloat16 [4096, 16384], P(None, 'tp')
- w_down: bfloat16 [16384, 4096], P('tp')
- grad_out: bfloat16 [32, 256, 4096], P('dp')
Outputs:
- output 1: bfloat16 [32, 256, 4096], P('dp')
- output 2: bfloat16 [4096, 32, 384], P('dp', 'tp')
- output 3: bfloat16 [4096, 4096], P(('dp', 'tp'))
- output 4: bfloat16 [4096, 16384], P('dp', 'tp')
- output 5: bfloat16 [16384, 4096], P(('dp', 'tp'))
All inputs are finite; a program needn't handle non-finite values.
Results may differ from a plain program's by a relative error of at most 0.0114769.
Values are sent between devices in bfloat16 or wider.
A program may use at most 768 MiB of HBM per device.

v0:
```python
import jax
import jax.numpy as jnp
from jax import lax
from jax.sharding import PartitionSpec as P

LN_EPS = 1e-5
GELU_COEF = 0.7071067811865476
PDF_COEF = 0.3989422804014327


def attend_rows(qkv_rows, dout_rows):
    seq_len = qkv_rows.shape[1]
    q_per_group = dout_rows.shape[3]
    score_scale = qkv_rows.shape[-1] ** -0.5
    causal = lax.broadcasted_iota(jnp.int32, (seq_len, seq_len), 0) >= lax.broadcasted_iota(jnp.int32, (seq_len, seq_len), 1)

    def one_row(row_pair):
        qkv_row, dout_row = row_pair
        q_row = qkv_row[:, :, :q_per_group]
        k_row = qkv_row[:, :, q_per_group]
        v_row = qkv_row[:, :, q_per_group + 1]
        scores = jnp.einsum('qgpd,kgd->gpqk', q_row, k_row, preferred_element_type=jnp.float32) * score_scale
        soft_probs = jax.nn.softmax(jnp.where(causal, scores, -1e30), axis=-1)
        probs_bf = soft_probs.astype(jnp.bfloat16)
        attn_out = jnp.einsum('gpqk,kgd->qgpd', probs_bf, v_row, preferred_element_type=jnp.float32).astype(jnp.bfloat16)
        d_probs = jnp.einsum('qgpd,kgd->gpqk', dout_row, v_row, preferred_element_type=jnp.float32)
        d_val = jnp.einsum('gpqk,qgpd->kgd', probs_bf, dout_row, preferred_element_type=jnp.float32)
        row_dot = jnp.sum(soft_probs * d_probs, axis=-1, keepdims=True)
        d_scores = (soft_probs * (d_probs - row_dot) * score_scale).astype(jnp.bfloat16)
        d_query = jnp.einsum('gpqk,kgd->qgpd', d_scores, k_row, preferred_element_type=jnp.float32)
        d_key = jnp.einsum('gpqk,qgpd->kgd', d_scores, q_row, preferred_element_type=jnp.float32)
        d_qkv = jnp.concatenate([d_query, d_key[:, :, None], d_val[:, :, None]], axis=2)
        return attn_out, d_qkv.astype(jnp.bfloat16)

    return lax.map(one_row, (qkv_rows, dout_rows))


def norm_stats(x_flat):
    x_f32 = x_flat.astype(jnp.float32)
    centered = x_f32 - jnp.mean(x_f32, axis=-1, keepdims=True)
    inv_std = lax.rsqrt(jnp.mean(centered * centered, axis=-1, keepdims=True) + LN_EPS)
    return centered * inv_std, inv_std


def finish_norm(norm_total, x_hat, inv_std, ln_gain, dy_flat):
    d_hat = norm_total * ln_gain
    grad_x = inv_std * (d_hat - jnp.mean(d_hat, axis=-1, keepdims=True) - x_hat * jnp.mean(d_hat * x_hat, axis=-1, keepdims=True))
    return (dy_flat.astype(jnp.float32) + grad_x).astype(jnp.bfloat16)


def branch_grads(tokens, ln_gain, ln_bias, w_qkv, w_out, w_up, w_down, grad_out):
    num_rows, seq_len, model_dim = tokens.shape
    tok_count = num_rows * seq_len
    groups = w_qkv.shape[1]
    per_group = w_qkv.shape[2]
    q_width = w_out.shape[0] // groups
    head_dim = (per_group - q_width) // 2
    q_per_group = q_width // head_dim
    dy_flat = grad_out.reshape(tok_count, model_dim)
    x_hat, inv_std = norm_stats(tokens.reshape(tok_count, model_dim))
    normed = (x_hat * ln_gain + ln_bias).astype(jnp.bfloat16)
    qkv_proj = jnp.einsum('th,hgc->tgc', normed, w_qkv, preferred_element_type=jnp.float32).astype(jnp.bfloat16)
    d_attn = jnp.einsum('th,ch->tc', dy_flat, w_out, preferred_element_type=jnp.float32).astype(jnp.bfloat16)
    attn_out, d_qkv = attend_rows(qkv_proj.reshape(num_rows, seq_len, groups, q_per_group + 2, head_dim), d_attn.reshape(num_rows, seq_len, groups, q_per_group, head_dim))
    attn_flat = attn_out.reshape(tok_count, groups * q_width)
    d_qkv_flat = d_qkv.reshape(tok_count, groups, per_group)
    hidden = jnp.dot(normed, w_up, preferred_element_type=jnp.float32)
    gauss_cdf = 0.5 * (1.0 + lax.erf(hidden * GELU_COEF))
    gelu_out = (hidden * gauss_cdf).astype(jnp.bfloat16)
    d_act = jnp.einsum('th,fh->tf', dy_flat, w_down, preferred_element_type=jnp.float32)
    d_hidden = (d_act * (gauss_cdf + hidden * PDF_COEF * jnp.exp(-0.5 * hidden * hidden))).astype(jnp.bfloat16)
    grad_qkv = jnp.einsum('th,tgc->hgc', normed, d_qkv_flat, preferred_element_type=jnp.float32)
    grad_wout = jnp.einsum('tc,th->ch', attn_flat, dy_flat, preferred_element_type=jnp.float32)
    grad_up = jnp.einsum('th,tf->hf', normed, d_hidden, preferred_element_type=jnp.float32)
    grad_down = jnp.einsum('tf,th->fh', gelu_out, dy_flat, preferred_element_type=jnp.float32)
    part_norm = jnp.einsum('tgc,hgc->th', d_qkv_flat, w_qkv, preferred_element_type=jnp.float32) + jnp.einsum('tf,hf->th', d_hidden, w_up, preferred_element_type=jnp.float32)
    return part_norm, x_hat, inv_std, dy_flat, (grad_qkv, grad_wout, grad_up, grad_down)


def solution(mesh):
    row_spec = P('dp', None, None)
    in_specs = (row_spec, P(None), P(None), P(None, 'tp', None), P('tp', None), P(None, 'tp'), P('tp', None), row_spec)
    out_specs = (row_spec, P('dp', 'tp', None), P(('dp', 'tp'), None), P('dp', 'tp'), P(('dp', 'tp'), None))

    def device_step(tokens, ln_gain, ln_bias, w_qkv, w_out, w_up, w_down, grad_out):
        part_norm, x_hat, inv_std, dy_flat, weight_grads = branch_grads(tokens, ln_gain, ln_bias, w_qkv, w_out, w_up, w_down, grad_out)
        norm_total = lax.psum(part_norm.astype(jnp.bfloat16), 'tp').astype(jnp.float32)
        grad_in = finish_norm(norm_total, x_hat, inv_std, ln_gain, dy_flat).reshape(tokens.shape)
        return (grad_in,) + tuple(grad_f32.astype(jnp.bfloat16) for grad_f32 in weight_grads)

    return jax.shard_map(device_step, mesh=mesh, in_specs=in_specs, out_specs=out_specs, check_vma=False)
```

profile of v0, /device:TPU:97, one launch (start us, length us, event | category | flops | bytes accessed | tf_op | source)
XLA Modules:
  0.0 1343.8 jit_solution(13790288234657061583)
XLA Ops:
  7.3 20.9 %convert_reduce_fusion = f32[32,256]{1,0:T(8,128)S(1)} fusion(bf16[32,256,4096]{2,1,0:T(8,128)(2,1)} %param.10), kind=kLoop, calls=%fused_computation.47 | loop fusion | flops 67100672 | bytes 67141632 | tf_op jit(solution)/shard_map/reduce_sum | solution.py:40
  28.9 24.1 %multiply_reduce_fusion.2 = f32[32,256]{1,0:T(8,128)S(1)} fusion(bf16[32,256,4096]{2,1,0:T(8,128)(2,1)} %param.10, f32[32,256]{1,0:T(8,128)S(1)} %get-tuple-element.81), kind=kLoop, calls=%fused_computation.46 | loop fusion | flops 134209536 | bytes 67174400 | tf_op jit(solution)/shard_map/reduce_sum | solution.py:41
  53.6 44.7 %add_convert_fusion.3 = bf16[32,256,4096]{2,1,0:T(8,128)(2,1)} fusion(bf16[32,256,4096]{2,1,0:T(8,128)(2,1)} %param.10, f32[4096]{0:T(1024)S(1)} %copy-done.12, f32[4096]{0:T(1024)S(1)} %copy-done.8, f32[32,256]{1,0:T(8,128)S(1)} %get-tuple-element.79, f32[32,256]{1,0:T(8,128)S(1)} %get-tuple-element.81), kind=kLoop, calls=%fused_computation.45 | loop fusion | flops 201326592 | bytes 134316032 | tf_op jit(solution)/shard_map/convert_element_type | solution.py:61
  98.3 41.2 %convolution_convert_fusion.4 = bf16[8192,384]{1,0:T(8,128)(2,1)} fusion(bf16[8192,4096]{1,0:T(8,128)(2,1)} %bitcast.1, bf16[4096,1,384]{2,0,1:T(8,128)(2,1)S(1)} %copy-done), kind=kOutput, calls=%fused_computation.56 | convolution fusion | flops 25772949504 | bytes 76546048 | tf_op jit(solution)/shard_map/th,hgc->tgc/dot_general | solution.py:62
  139.5 16.6 %reshape.257 = bf16[32,256,1,3,128]{4,3,1,0,2:T(4,128)(2,1)} reshape(bf16[8192,384]{1,0:T(8,128)(2,1)} %convolution_convert_fusion.4) | data formatting | bytes 12582912 | tf_op jit(solution)/shard_map/reshape | solution.py:64
  156.1 7.9 copy.16
  164.0 28.9 %convolution_convert_fusion.5 = bf16[8192,128]{1,0:T(8,128)(2,1)} fusion(bf16[8192,4096]{1,0:T(8,128)(2,1)} %bitcast, bf16[128,4096]{1,0:T(8,128)(2,1)} %param.14), kind=kOutput, calls=%fused_computation.57 | convolution fusion | flops 8590983168 | bytes 70254592 | tf_op jit(solution)/shard_map/th,ch->tc/dot_general | solution.py:63
  192.9 300.0 %while.13 = (s32[]{:T(128)}, bf16[32,256,1,1,128]{4,1,0,3,2:T(8,128)(2,1)}, bf16[32,256,1,3,128]{1,4,3,2,0:T(8,128)(2,1)}, bf16[32,256,1,3,128]{4,1,3,2,0:T(8,12...) while((s32[]{:T(128)}, bf16[32,256,1,1,128]{4,1,0,3,2:T(8,128)(2,1)}, ...), condition=%wide.region_6.7_spmd.clone, body=%wide.region_2.6_spmd.clone.sunk | while | flops 102825216 | bytes 5133493 | solution.py:35
  194.2 1.7 fusion.81
  203.5 1.7 fusion.81
  222.3 1.7 fusion.81
  231.6 1.7 fusion.81
  241.0 1.7 fusion.81
  250.4 1.7 fusion.81
  259.7 1.7 fusion.81
  269.1 1.7 fusion.81
  287.8 1.7 fusion.81
  297.2 1.7 fusion.81
  306.6 1.7 fusion.81
  325.3 1.7 fusion.81
  334.7 1.7 fusion.81
  344.1 1.7 fusion.81
  353.4 1.7 fusion.81
  381.5 1.7 fusion.81
  390.9 1.7 fusion.81
  400.3 1.7 fusion.81
  409.6 1.7 fusion.81
  419.0 1.7 fusion.81
  428.4 1.7 fusion.81
  447.1 1.7 fusion.81
  456.5 1.7 fusion.81
  465.9 1.7 fusion.81
  475.2 1.7 fusion.81
  484.6 1.7 fusion.81
  492.9 6.4 copy.18
  499.3 10.2 copy.25
  509.4 49.4 %fusion.34 = f32[8192,4096]{1,0:T(8,128)} fusion(bf16[8192,384]{0,1:T(8,128)(2,1)} %bitcast.164, bf16[4096,1,384]{2,0,1:T(8,128)(2,1)S(1)} %copy-done), kind=kOutput, calls=%fused_computation.64 | convolution fusion | flops 25769803776 | bytes 143654912 | tf_op jit(solution)/shard_map/tgc,hgc->th/dot_general | solution.py:76
  558.9 44.6 %add_convert_fusion.2 = bf16[8192,4096]{1,0:T(8,128)(2,1)} fusion(bf16[32,256,4096]{2,1,0:T(8,128)(2,1)} %param.10, f32[4096]{0:T(1024)S(1)} %copy-done.13, f32[4096]{0:T(1024)S(1)} %copy-done.8, f32[8192]{0:T(1024)S(1)} %bitcast.168, f32[8192]{0:T(1024)S(1)} %bitcast.171), kind=kLoop, calls=%fused_computation.44 | loop fusion | flops 201326592 | bytes 134316032 | tf_op jit(solution)/shard_map/convert_element_type | solution.py:61
  603.5 42.9 %fusion.40 = f32[8192,512]{1,0:T(8,128)} fusion(bf16[8192,4096]{1,0:T(8,128)(2,1)} %add_convert_fusion.2, bf16[4096,512]{1,0:T(8,128)(2,1)} %param.15), kind=kOutput, calls=%fused_computation.74 | convolution fusion | flops 34359738368 | bytes 88080384 | tf_op jit(solution)/shard_map/dot_general | solution.py:67
  646.4 50.0 %fusion.30 = bf16[8192,512]{1,0:T(8,128)(2,1)} fusion(f32[8192,512]{1,0:T(8,128)} %fusion.40, bf16[8192,4096]{1,0:T(8,128)(2,1)} %bitcast, bf16[512,4096]{1,0:T(8,128)(2,1)} %param.16), kind=kOutput, calls=%fused_computation.53 | convolution fusion | flops 34401681408 | bytes 96468992 | tf_op jit(solution)/shard_map/th,fh->tf/dot_general | solution.py:70
  696.5 72.4 %add_convert_fusion.1 = bf16[8192,4096]{1,0:T(8,128)(2,1)} fusion(f32[8192,4096]{1,0:T(8,128)} %fusion.34, bf16[8192,512]{1,0:T(8,128)(2,1)} %fusion.30, bf16[4096,512]{1,0:T(8,128)(2,1)} %param.15), kind=kOutput, calls=%fused_computation.43 | convolution fusion | flops 34426847232 | bytes 213909504 | tf_op jit(solution)/shard_map/tf,hf->th/dot_general | solution.py:76
  770.5 24.8 %convolution_convert_fusion.8 = bf16[128,4096]{1,0:T(8,128)(2,1)} fusion(bf16[8192,128]{1,0:T(8,128)(2,1)S(1)} %bitcast.167, bf16[8192,4096]{1,0:T(8,128)(2,1)} %bitcast), kind=kOutput, calls=%fused_computation.63 | convolution fusion | flops 8590458880 | bytes 70254592 | tf_op jit(solution)/shard_map/tc,th->ch/dot_general | solution.py:73
  795.3 44.5 %convolution_convert_fusion.6 = bf16[4096,512]{1,0:T(8,128)(2,1)} fusion(bf16[8192,4096]{1,0:T(8,128)(2,1)} %add_convert_fusion.2, bf16[8192,512]{1,0:T(8,128)(2,1)} %fusion.30), kind=kOutput, calls=%fused_computation.60 | convolution fusion | flops 34361835520 | bytes 79691776 | tf_op jit(solution)/shard_map/th,tf->hf/dot_general | solution.py:74
  839.8 44.4 %fusion.32 = bf16[512,4096]{1,0:T(8,128)(2,1)} fusion(bf16[8192,4096]{1,0:T(8,128)(2,1)} %bitcast, f32[8192,512]{1,0:T(8,128)} %fusion.40), kind=kOutput, calls=%fused_computation.59 | convolution fusion | flops 34382807040 | bytes 88080384 | tf_op jit(solution)/shard_map/tf,th->fh/dot_general | solution.py:75
  884.2 44.1 %fusion.33 = bf16[4096,1,384]{2,0,1:T(8,128)(2,1)} fusion(bf16[8192,4096]{1,0:T(8,128)(2,1)} %bitcast.1, bf16[8192,384]{0,1:T(8,128)(2,1)} %bitcast.165), kind=kOutput, calls=%fused_computation.62 | convolution fusion | flops 25771376640 | bytes 76546048 | tf_op jit(solution)/shard_map/th,tgc->hgc/dot_general | solution.py:72
  928.3 279.4 %all-reduce.2.cloned.1.call-done = bf16[8192,4096]{1,0:T(8,128)(2,1)} async-done(((bf16[8192,4096]{1,0:T(8,128)(2,1)}), bf16[8192,4096]{1,0:T(8,128)(2,1)}) %all-reduce.2.cloned.1.call-update) | async-done | bytes 67108880 | tf_op jit(solution)/shard_map/psum | solution.py:87
  1207.7 43.5 %fusion.25 = (f32[8192]{0:T(1024)S(1)}, f32[8192]{0:T(1024)S(1)}) fusion(bf16[8192,4096]{1,0:T(8,128)(2,1)} %all-reduce.2.cloned.1.call-done, f32[4096]{0:T(1024)S(1)} %copy-done.9, f32[8192]{0:T(1024)S(1)} %bitcast.172, f32[8192]{0:T(1024)S(1)} %bitcast.169, bf16[32,256,4096]{2,1,0:T(8,128)(2,1)} %param.10), kind=kLoop, calls=%fused_computation.42 | loop fusion | flops 268419072 | bytes 134365184 | tf_op jit(solution)/shard_map/reduce_sum | solution.py:47
  1251.3 85.2 %add_convert_fusion = bf16[8192,4096]{1,0:T(8,128)(2,1)} fusion(bf16[8192,4096]{1,0:T(8,128)(2,1)} %all-reduce.2.cloned.1.call-done, bf16[32,256,4096]{2,1,0:T(8,128)(2,1)} %param.10, f32[8192]{0:T(1024)S(1)} %get-tuple-element.82, f32[8192]{0:T(1024)S(1)} %get-tuple-element.83, f32[4096]{0:T(1024)S(1)} %copy-done.9, f32[8192]{0:T(1024)S(1)} %bitcast.170, ...), kind=kLoop, calls=%fused_computation.39 | loop fusion | flops 402653184 | bytes 268582912 | tf_op jit(solution)/shard_map/convert_element_type | solution.py:48
  (581 shorter events, 257.2 us)
Async XLA Ops:
  7.2 91.1 %copy-start = (bf16[4096,1,384]{2,0,1:T(8,128)(2,1)S(1)}, bf16[4096,1,384]{2,0,1:T(8,128)(2,1)}, u32[]{:S(2)}) copy-start(bf16[4096,1,384]{2,0,1:T(8,128)(2,1)} %param.13) | copy-start | bytes 9437188
  7.2 1200.5 %all-reduce.2.cloned.1.call-start = ((), (), s32[]{:S(2)}) async-start(), calls=%async_computation | async-start | bytes 134217728 | tf_op jit(solution)/shard_map/psum | solution.py:87
  28.8 24.8 %copy-start.8 = (f32[4096]{0:T(1024)S(1)}, f32[4096]{0:T(1024)}, u32[]{:S(2)}) copy-start(f32[4096]{0:T(1024)} %param.11) | copy-start | bytes 49156
  28.8 24.8 %copy-start.12 = (f32[4096]{0:T(1024)S(1)}, f32[4096]{0:T(1024)}, u32[]{:S(2)}) copy-start(f32[4096]{0:T(1024)} %param.12) | copy-start | bytes 49156
  193.8 2.0 copy-start.2
  203.2 2.0 copy-start.2
  203.4 1.8 copy-start.10
  212.6 2.0 copy-start.2
  222.0 2.0 copy-start.2
  222.2 1.8 copy-start.10
  231.3 2.0 copy-start.2
  240.7 2.0 copy-start.2
  250.1 2.0 copy-start.2
  259.4 2.0 copy-start.2
  268.8 2.0 copy-start.2
  278.2 2.0 copy-start.2
  287.5 2.0 copy-start.2
  296.9 2.0 copy-start.2
  306.3 2.0 copy-start.2
  306.5 1.8 copy-start.10
  315.6 2.0 copy-start.2
  325.0 2.0 copy-start.2
  325.2 1.8 copy-start.10
  334.4 2.0 copy-start.2
  334.6 1.8 copy-start.10
  343.7 2.0 copy-start.2
  353.1 2.0 copy-start.2
  362.5 2.0 copy-start.2
  371.8 2.0 copy-start.2
  381.2 2.0 copy-start.2
  390.6 2.0 copy-start.2
  400.0 2.0 copy-start.2
  409.3 2.0 copy-start.2
  418.7 2.0 copy-start.2
  428.1 2.0 copy-start.2
  437.4 2.0 copy-start.2
  446.8 2.0 copy-start.2
  456.2 2.0 copy-start.2
  465.5 2.0 copy-start.2
  474.9 2.0 copy-start.2
  484.3 2.0 copy-start.2
  509.4 49.5 %copy-start.4 = (f32[4,2,8,128]{3,1,2,0:T(2,128)S(1)}, f32[4,2,8,128]{3,1,2,0:T(2,128)}, u32[]{:S(2)}) copy-start(f32[4,2,8,128]{3,1,2,0:T(2,128)} %copy.26) | copy-start | bytes 98308
  509.4 49.5 %copy-start.6 = (f32[4,2,8,128]{3,1,2,0:T(2,128)S(1)}, f32[4,2,8,128]{3,1,2,0:T(2,128)}, u32[]{:S(2)}) copy-start(f32[4,2,8,128]{3,1,2,0:T(2,128)} %copy.24) | copy-start | bytes 98308
  509.4 49.5 %copy-start.13 = (f32[4096]{0:T(1024)S(1)}, f32[4096]{0:T(1024)}, u32[]{:S(2)}) copy-start(f32[4096]{0:T(1024)} %param.12) | copy-start | bytes 49156
  884.2 323.5 %copy-start.5 = (f32[4,2,8,128]{3,1,2,0:T(2,128)S(1)}, f32[4,2,8,128]{3,1,2,0:T(2,128)}, u32[]{:S(2)}) copy-start(f32[4,2,8,128]{3,1,2,0:T(2,128)} %copy.26) | copy-start | bytes 98308
  884.2 323.5 %copy-start.7 = (f32[4,2,8,128]{3,1,2,0:T(2,128)S(1)}, f32[4,2,8,128]{3,1,2,0:T(2,128)}, u32[]{:S(2)}) copy-start(f32[4,2,8,128]{3,1,2,0:T(2,128)} %copy.24) | copy-start | bytes 98308
  884.2 323.5 %copy-start.9 = (f32[4096]{0:T(1024)S(1)}, f32[4096]{0:T(1024)}, u32[]{:S(2)}) copy-start(f32[4096]{0:T(1024)} %param.11) | copy-start | bytes 49156
  1251.3 85.3 %copy-start.1 = (bf16[4096,1,384]{2,0,1:T(8,128)(2,1)S(1)}, bf16[4096,1,384]{2,0,1:T(8,128)(2,1)}, u32[]{:S(2)}) copy-start(bf16[4096,1,384]{2,0,1:T(8,128)(2,1)} %param.13) | copy-start | bytes 9437188
  (60 other events, 103.9 us)
Sparse Core Ops, SparseCore 0:
  769.1 438.5 all-reduce.1
where the time goes:
time: 1360 us; the launch traced here: 1340 us
  matrix products  611 us (45%)
  other arithmetic  338 us (25%)
  waiting for transfers between devices  279 us (21%)
  local copies, waits for them, and re-layouts  98.7 us (7%)
  between operations  14.6 us (1%)
    psum x1, waiting for transfers between devices, device_step(): lax.psum(part_norm.astype(jnp.bfloat16), 'tp').astype(jnp.float32)  279 us
    convert_element_type x2, other arithmetic, branch_grads(): normed = (x_hat * ln_gain + ln_bias).astype(jnp.bfloat16)  89.4 us
    convert_element_type x1, other arithmetic, finish_norm(): return (dy_flat.astype(jnp.float32) + grad_x).astype(jnp.bfloat16)  85.2 us
    dot_general x1, matrix products, branch_grads(): jnp.einsum('tf,hf->th', d_hidden, w_up, preferred_element_type=jnp.float32)  72.4 us
    dot_general x32, matrix products, one_row(): jnp.einsum('gpqk,qgpd->kgd', probs_bf, dout_row, preferred_element_type=j...  54 us
    dot_general x1, matrix products, branch_grads(): jnp.einsum('th,fh->tf', dy_flat, w_down, preferred_element_type=jnp.float32)  50 us
    dot_general x1, matrix products, branch_grads(): jnp.einsum('tgc,hgc->th', d_qkv_flat, w_qkv, preferred_element_type=jnp.f...  49.4 us
    dynamic_update_slice x32, other arithmetic, attend_rows(): return lax.map(one_row, (qkv_rows, dout_rows))  49 us
  transfers between devices with their start and end apart: 1, of which 1 were waited for; matrix products, arithmetic and copies ran while one was open for 12% of the time, Pallas kernels for 0%

commit v1 on v0

v1 whole, which is shorter than its diff:
```python
import functools
import jax
import jax.numpy as jnp
from jax import lax
from jax.experimental import pallas as pl
from jax.experimental.pallas import tpu as pltpu
from jax.sharding import PartitionSpec as P

EPS = 1e-5
GELU_COEF = 0.7071067811865476
PDF_COEF = 0.3989422804014327
F32 = jnp.float32
BF = jnp.bfloat16
VMEM_LIMIT = 64 * 2**20 - 65536
CORES = 2
COLORS = 4


def dg(a, b, ca, cb):
    return lax.dot_general(a, b, (((ca,), (cb,)), ((), ())), preferred_element_type=F32)


def normalize(x):
    x = x.astype(F32)
    c = x - jnp.mean(x, axis=-1, keepdims=True)
    r = lax.rsqrt(jnp.mean(c * c, axis=-1, keepdims=True) + EPS)
    return c * r, r


def attend(q, k, v, do, scale):
    S = q.shape[1]
    st = dg(k, q, 0, 0) * scale
    ki = lax.broadcasted_iota(jnp.int32, (S, S), 0)
    qi = lax.broadcasted_iota(jnp.int32, (S, S), 1)
    st = jnp.where(ki <= qi, st, -1e30)
    e = jnp.exp(st - jnp.max(st, axis=0, keepdims=True))
    p = e / jnp.sum(e, axis=0, keepdims=True)
    pb = p.astype(BF)
    o = dg(v, pb, 1, 0)
    dp = dg(v, do, 0, 0)
    dv = dg(do, pb, 1, 1)
    rd = jnp.sum(p * dp, axis=0, keepdims=True)
    ds = (p * (dp - rd) * scale).astype(BF)
    dq = dg(k, ds, 1, 0)
    dk = dg(q, ds, 1, 1)
    return o.astype(BF), dq.astype(BF), dk.astype(BF), dv.astype(BF)


class Place:
    def __init__(self, axis, side):
        self.axis, self.side = axis, side
        i = lax.axis_index(axis)
        self.c = lax.rem(i, CORES)
        chip = lax.div(i, CORES)
        self.x = lax.rem(chip, side)
        self.y = lax.div(chip, side)

    def index(self, x, y, c):
        return (y * self.side + x) * CORES + c

    def step(self, along, by):
        n = self.side
        if along == "x":
            return self.index(lax.rem(self.x + by + n, n), self.y, self.c)
        return self.index(self.x, lax.rem(self.y + by + n, n), self.c)

    def peer(self):
        return self.index(self.x, self.y, 1 - self.c)

    def block(self, along, by):
        n = self.side
        return lax.rem((self.x if along == "x" else self.y) + by + 2 * n, n)

    def partners(self):
        return [self.step("x", 1), self.step("x", -1), self.step("y", 1), self.step("y", -1), self.peer()]

    def greet(self):
        sem = pltpu.get_barrier_semaphore()
        who = self.partners()
        for w in who:
            pl.semaphore_signal(sem, inc=1, device_id={self.axis: w}, device_id_type=pl.DeviceIdType.MESH)
        pl.semaphore_wait(sem, len(who))


RINGS = (("x", "y", 1), ("x", "y", -1), ("y", "x", 1), ("y", "x", -1))


def forward_kernel(axis, side, S, d, C, F, nt, NB,
                   x0_ref, x_ref, dy_ref, g_ref, b_ref, wt_ref, wd_ref, xh_ref, dyh_ref,
                   lnh_ref, dc_ref, og_ref, sh_ref,
                   ln_s, h_s, da_s, qkv_s, do_s, dct_s, p_s, q_s, r1_s, r2_s, fx_s, fd_s, fo_s,
                   ln_sem, s0_send, s0_recv, s1_send, s1_recv, s2_send, s2_recv, f_sem, fo_sem):
    TM, D = x_ref.shape
    n = side
    me = Place(axis, side)
    g = pl.program_id(0)
    slot = lax.rem(g, 2)
    nxt = 1 - slot
    nu = nt // 2
    CW = D // COLORS
    QB = q_s.shape[0]
    RB = r1_s.shape[0]
    RR = q_s.shape[3]

    def copy_to(src, dst, ssem, rsem, dev):
        return pltpu.make_async_remote_copy(src_ref=src, dst_ref=dst, send_sem=ssem, recv_sem=rsem,
                                            device_id={axis: dev}, device_id_type=pl.DeviceIdType.MESH)

    def cols(k):
        return pl.ds(k * CW, CW)

    def st0(u):
        return copy_to(p_s.at[lax.rem(u, 2), 1 - me.c], q_s.at[lax.rem(u, QB)], s0_send.at[lax.rem(u, QB)], s0_recv.at[lax.rem(u, QB)], me.peer())

    def q_block(u, k, by):
        along = RINGS[k][0]
        q = q_s.at[lax.rem(u, QB)]
        b = me.block(along, by)
        return q.at[b, :, :, cols(k)] if along == "x" else q.at[:, b, :, cols(k)]

    def st1(u, k, s):
        along, _, sg = RINGS[k]
        rs = lax.rem(u, RB)
        src = q_block(u, k, -sg) if s == 0 else r1_s.at[rs, s - 1, k]
        return copy_to(src, r1_s.at[rs, s, k], s1_send.at[rs, s, k], s1_recv.at[rs, s, k], me.step(along, sg))

    def st2(u, k, s):
        _, along, sg = RINGS[k]
        rs = lax.rem(u, RB)
        src = r1_s.at[rs, n - 2, k, me.block(along, -sg)] if s == 0 else r2_s.at[rs, s - 1, k]
        return copy_to(src, r2_s.at[rs, s, k], s2_send.at[rs, s, k], s2_recv.at[rs, s, k], me.step(along, sg))

    def on_st0(u):
        st0(u).wait()
        qi, pi = lax.rem(u, QB), lax.rem(u, 2)

        def add(i, _):
            a, b = lax.div(i, n), lax.rem(i, n)
            q_s[qi, a, b] = q_s[qi, a, b] + p_s[pi, me.c, a, b]
            return 0
        lax.fori_loop(0, n * n, add, 0)
        for k in range(COLORS):
            st1(u, k, 0).start()

    def on_st1(u, s):
        for k in range(COLORS):
            st1(u, k, s).wait()
        rs = lax.rem(u, RB)
        for k in range(COLORS):
            sg = RINGS[k][2]
            own = q_block(u, k, -sg * (2 + s))

            def add(i, _, k=k, own=own):
                r1_s[rs, s, k, i] = r1_s[rs, s, k, i] + own[i]
                return 0
            lax.fori_loop(0, n, add, 0)
        for k in range(COLORS):
            (st1(u, k, s + 1) if s < n - 2 else st2(u, k, 0)).start()

    def shard_rows(u):
        r = u * 2 * TM + ((me.c * n + me.x) * n + me.y) * RR
        return pl.ds(pl.multiple_of(r, RR), RR)

    def fetch(u):
        return (pltpu.make_async_copy(xh_ref.at[shard_rows(u), :], fx_s, f_sem.at[0]),
                pltpu.make_async_copy(dyh_ref.at[shard_rows(u), :], fd_s, f_sem.at[1]))

    def put(u):
        return pltpu.make_async_copy(fo_s, sh_ref.at[u], fo_sem)

    def on_st2(u, s):
        for k in range(COLORS):
            st2(u, k, s).wait()
        rs = lax.rem(u, RB)
        for k in range(COLORS):
            along, sg = RINGS[k][1], RINGS[k][2]
            own = r1_s.at[rs, n - 2, k, me.block(along, -sg * (2 + s))]
            r2_s[rs, s, k] = r2_s[rs, s, k] + own[...]
            if s < n - 2:
                st2(u, k, s + 1).start()
        if s == n - 3:
            for f in fetch(u):
                f.start()
        if s == n - 2:
            for f in fetch(u):
                f.wait()

            @pl.when(u > 0)
            def _():
                put(u - 1).wait()
            xhat, r = normalize(fx_s[...])
            total = jnp.concatenate([r2_s[rs, s, k] for k in range(COLORS)], axis=-1).astype(F32)
            dh = total * g_ref[...]
            gx = r * (dh - jnp.mean(dh, axis=-1, keepdims=True) - xhat * jnp.mean(dh * xhat, axis=-1, keepdims=True))
            fo_s[...] = (fd_s[...].astype(F32) + gx).astype(BF)
            put(u).start()

            @pl.when(u == nu - 1)
            def _():
                put(u).wait()

    events = {2: on_st0}
    for s in range(n - 1):
        events[2 + 3 * (s + 1)] = functools.partial(on_st1, s=s)
        events[2 + 3 * (s + n)] = functools.partial(on_st2, s=s)

    def comm(r):
        for rho, fn in events.items():
            if rho % 4 != r:
                continue
            back = 2 + rho // 4
            u = lax.div(g - back, 2)

            @pl.when((g >= back) & (lax.rem(g - back + 2 * nt, 2) == 0) & (u < nu))
            def _():
                fn(u)

    def ln_block(src, dst_slot, r0, m):
        rows = pl.ds(pl.multiple_of(r0, m), m)
        xhat, _ = normalize(src[rows, :])
        ln_s[dst_slot, rows, :] = (xhat * g_ref[...] + b_ref[...]).astype(BF)

    def out_copy(sl, tt):
        return pltpu.make_async_copy(ln_s.at[sl], lnh_ref.at[pl.ds(pl.multiple_of(tt * TM, TM), TM), :], ln_sem.at[sl])

    @pl.when(g == 0)
    def _():
        me.greet()

        def lnb(i, _):
            ln_block(x0_ref, 0, i * 16, 16)
            return 0
        lax.fori_loop(0, TM // 16, lnb, 0)

    live = g < nt

    @pl.when((g > 0) & (g <= nt))
    def _():
        out_copy(nxt, g - 1).wait()

    comm(0)

    @pl.when(live)
    def _():
        out_copy(slot, g).start()
        lns = ln_s.at[slot]
        qkv_s[...] = dg(wt_ref[:C, :], lns[...], 1, 1).astype(BF)
        y = dg(wd_ref[:d + F // 2, :], dy_ref[...], 1, 1)
        do_s[...] = y[:d].astype(BF)
        da_s[:F // 2, :] = y[d:]

    comm(1)

    @pl.when(live)
    def _():
        lns = ln_s.at[slot]
        h_s[:F // 2, :] = dg(wt_ref[C:C + F // 2, :], lns[...], 1, 1)
        da_s[F // 2:, :] = dg(wd_ref[d + F // 2:, :], dy_ref[...], 1, 1)
        h_s[F // 2:, :] = dg(wt_ref[C + F // 2:, :], lns[...], 1, 1)
        for s in range(TM // S):
            cs = slice(s * S, (s + 1) * S)
            o, dq, dk, dv = attend(qkv_s[:d, cs], qkv_s[d:2 * d, cs], qkv_s[2 * d:3 * d, cs], do_s[:, cs], d ** -0.5)
            og_ref[:d, cs] = o
            dc_ref[:d, cs] = dq
            dc_ref[d:2 * d, cs] = dk
            dc_ref[2 * d:3 * d, cs] = dv

    comm(2)

    nsteps = D // NB
    LR = TM // nsteps
    uslot = lax.rem(lax.div(g, 2), 2)

    def c_block(i, _):
        cs = pl.ds(pl.multiple_of(i * NB, NB), NB)
        res = dg(dct_s[...], wt_ref[:, cs], 1, 0).astype(BF)
        p_s[uslot, slot, :, :, :, cs] = res.reshape(n, n, RR, NB)
        for j in range(LR // 16):
            ln_block(x_ref, nxt, i * LR + j * 16, 16)
        return 0

    @pl.when(live)
    def _():
        def gb(i, _):
            r = pl.ds(pl.multiple_of(i * 16, 16), 16)
            h = h_s[r, :]
            cdf = 0.5 * (1.0 + lax.erf(h * GELU_COEF))
            og_ref[pl.ds(pl.multiple_of(d + i * 16, 16), 16), :] = (h * cdf).astype(BF)
            dc_ref[pl.ds(pl.multiple_of(C + i * 16, 16), 16), :] = (da_s[r, :] * (cdf + h * PDF_COEF * jnp.exp(-0.5 * h * h))).astype(BF)
            return 0
        lax.fori_loop(0, F // 16, gb, 0, unroll=2)
        dct_s[...] = dc_ref[...].T
        lax.fori_loop(0, nsteps // 2, c_block, 0)

    comm(3)

    @pl.when(live)
    def _():
        lax.fori_loop(nsteps // 2, nsteps, c_block, 0)

    @pl.when(live & (slot == 1))
    def _():
        st0(lax.div(g, 2)).start()


def forward(axis, side, x, dy, gain, bias, wt, wd, S, TM=256, NB=1024):
    T, D = x.shape
    CF, dF = wt.shape[0], wd.shape[0]
    d = (CF - dF) // 2
    C = 3 * d
    F = CF - C
    nt = T // TM
    nu = nt // 2
    RR = 2 * TM // (CORES * side * side)
    drain = 2 + (2 + 3 * (2 * side - 2)) // 4 - 1
    CW = D // COLORS
    last = nt - 1
    QB, RB = 3, 4
    return pl.pallas_call(
        functools.partial(forward_kernel, axis, side, S, d, C, F, nt, NB),
        grid=(nt + drain,),
        in_specs=[pl.BlockSpec((TM, D), lambda t: (0, 0), pipeline_mode=pl.Buffered(1)),
                  pl.BlockSpec((TM, D), lambda t: (jnp.minimum(t + 1, last), 0)),
                  pl.BlockSpec((TM, D), lambda t: (jnp.minimum(t, last), 0)),
                  pl.BlockSpec((1, D), lambda t: (0, 0)),
                  pl.BlockSpec((1, D), lambda t: (0, 0)),
                  pl.BlockSpec((CF, D), lambda t: (0, 0), pipeline_mode=pl.Buffered(1)),
                  pl.BlockSpec((dF, D), lambda t: (0, 0), pipeline_mode=pl.Buffered(1)),
                  pl.BlockSpec(memory_space=pl.ANY),
                  pl.BlockSpec(memory_space=pl.ANY)],
        out_specs=[pl.BlockSpec(memory_space=pl.ANY),
                   pl.BlockSpec((CF, TM), lambda t: (0, jnp.minimum(t, last))),
                   pl.BlockSpec((dF, TM), lambda t: (0, jnp.minimum(t, last))),
                   pl.BlockSpec(memory_space=pl.ANY)],
        out_shape=[jax.ShapeDtypeStruct((T, D), BF), jax.ShapeDtypeStruct((CF, T), BF),
                   jax.ShapeDtypeStruct((dF, T), BF), jax.ShapeDtypeStruct((nu, RR, D), BF)],
        scratch_shapes=[pltpu.VMEM((2, TM, D), BF), pltpu.VMEM((F, TM), F32), pltpu.VMEM((F, TM), F32),
                        pltpu.VMEM((C, TM), BF), pltpu.VMEM((d, TM), BF), pltpu.VMEM((TM, CF), BF),
                        pltpu.VMEM((2, CORES, side, side, RR, D), BF),
                        pltpu.VMEM((QB, side, side, RR, D), BF),
                        pltpu.VMEM((RB, side - 1, COLORS, side, RR, CW), BF),
                        pltpu.VMEM((RB, side - 1, COLORS, RR, CW), BF),
                        pltpu.VMEM((RR, D), BF), pltpu.VMEM((RR, D), BF), pltpu.VMEM((RR, D), BF),
                        pltpu.SemaphoreType.DMA((2,)),
                        pltpu.SemaphoreType.DMA((QB,)), pltpu.SemaphoreType.DMA((QB,)),
                        pltpu.SemaphoreType.DMA((RB, side - 1, COLORS)), pltpu.SemaphoreType.DMA((RB, side - 1, COLORS)),
                        pltpu.SemaphoreType.DMA((RB, side - 1, COLORS)), pltpu.SemaphoreType.DMA((RB, side - 1, COLORS)),
                        pltpu.SemaphoreType.DMA((2,)), pltpu.SemaphoreType.DMA],
        compiler_params=pltpu.CompilerParams(vmem_limit_bytes=VMEM_LIMIT, collective_id=1, has_side_effects=True),
        name="forward_rs",
    )(x, x, dy, gain.reshape(1, D), bias.reshape(1, D), wt, wd, x, dy)


def gather_kernel(axis, side, NP, sh_ref, dc_ref, ln_ref, o_ref, g_ref, own_s, l_sem, snd, rcv, p_snd, p_rcv):
    n = side
    me = Place(axis, side)
    g = pl.program_id(0)
    ng = 8
    nu, RR, D = sh_ref.shape
    PU = nu // NP
    CW = D // COLORS
    HA = n - 1

    def copy_to(src, dst, ssem, rsem, dev):
        return pltpu.make_async_remote_copy(src_ref=src, dst_ref=dst, send_sem=ssem, recv_sem=rsem,
                                            device_id={axis: dev}, device_id_type=pl.DeviceIdType.MESH)

    def units(p):
        return pl.ds(p * PU, PU)

    def region(p, k, h, lag):
        along_b, along_a, sg = RINGS[k]
        cw = pl.ds(k * CW, CW)
        if h < HA:
            b = me.block(along_a, -sg * lag)
            xi, yi = (me.x, b) if along_a == "y" else (b, me.y)
            return g_ref.at[units(p), me.c, xi, yi, :, cw]
        b = me.block(along_b, -sg * lag)
        if along_b == "x":
            return g_ref.at[units(p), me.c, b, :, :, cw]
        return g_ref.at[units(p), me.c, :, b, :, cw]

    def hop(p, k, h):
        along_b, along_a, sg = RINGS[k]
        s = h if h < HA else h - HA
        dst = region(p, k, h, s)
        src = own_s.at[units(p), :, pl.ds(k * CW, CW)] if h == 0 else dst
        return copy_to(src, dst, snd.at[p, k, h], rcv.at[p, k, h], me.step(along_a if h < HA else along_b, sg))

    def to_peer(src, dst):
        return copy_to(src, dst, p_snd, p_rcv, me.peer())

    def arrived(p, h):
        for k in range(COLORS):
            hop(p, k, h).wait()
            if h < 2 * HA - 1:
                hop(p, k, h + 1).start()
            s = h if h < HA else h - HA
            got = region(p, k, h, s + 1)
            to_peer(got, got).start()

    def mine():
        return g_ref.at[:, me.c, me.x, me.y]

    @pl.when(g == 0)
    def _():
        me.greet()
        ld = pltpu.make_async_copy(sh_ref, own_s, l_sem)
        ld.start()
        ld.wait()
        for p in range(NP):
            for k in range(COLORS):
                hop(p, k, 0).start()
        pltpu.make_async_copy(own_s, mine(), l_sem).start()
        to_peer(own_s, mine()).start()

    M = dc_ref.shape[0]
    half = M // 2
    for j in range(2):
        rows = slice(j * half, (j + 1) * half)
        o_ref[rows, :] = jnp.dot(dc_ref[rows, :], ln_ref[...], preferred_element_type=F32).astype(BF)
        if j == 0:
            @pl.when(g == 0)
            def _():
                pltpu.make_async_copy(own_s, mine(), l_sem).wait()
        for h in range(HA):
            @pl.when(g == h)
            def _(h=h):
                arrived(2 * j, h)
                arrived(2 * j + 1, h)

        @pl.when((g == 3) | (g == 4))
        def _():
            arrived(2 * (g - 3) + j, 3)

        @pl.when(g == 5)
        def _():
            arrived(2 * j, 4)
            arrived(2 * j + 1, 4)

        @pl.when((g == 6) | (g == 7))
        def _():
            arrived(2 * (g - 6) + j, 5)

    @pl.when(g == ng - 1)
    def _():
        to_peer(g_ref.at[:, me.c], g_ref.at[:, me.c]).wait()


def gather(axis, side, sh, dc, ln, NB=512):
    nu, RR, D = sh.shape
    M, T = dc.shape
    NP = 4
    hops = 2 * (side - 1)
    return pl.pallas_call(
        functools.partial(gather_kernel, axis, side, NP),
        grid=(D // NB,),
        in_specs=[pl.BlockSpec(memory_space=pl.ANY),
                  pl.BlockSpec((M, T), lambda t: (0, 0), pipeline_mode=pl.Buffered(1)),
                  pl.BlockSpec((T, NB), lambda t: (0, t))],
        out_specs=[pl.BlockSpec((M, NB), lambda t: (0, t)), pl.BlockSpec(memory_space=pl.ANY)],
        out_shape=[jax.ShapeDtypeStruct((M, D), BF), jax.ShapeDtypeStruct((nu, CORES, side, side, RR, D), BF)],
        scratch_shapes=[pltpu.VMEM((nu, RR, D), BF), pltpu.SemaphoreType.DMA,
                        pltpu.SemaphoreType.DMA((NP, COLORS, hops)), pltpu.SemaphoreType.DMA((NP, COLORS, hops)),
                        pltpu.SemaphoreType.DMA, pltpu.SemaphoreType.DMA],
        compiler_params=pltpu.CompilerParams(vmem_limit_bytes=VMEM_LIMIT, collective_id=2, has_side_effects=True),
        name="gather_grads",
    )(sh, dc, ln)


def finish_kernel(d, C, og_ref, dy_ref, ot_ref, gh_ref, gw_ref, gd_ref, gq_ref, gu_ref, dx_ref, buf, isem, osem):
    g = pl.program_id(0)
    ng = pl.num_programs(0)
    R = buf.shape[1]

    def cin(a):
        return pltpu.make_async_copy(gh_ref.at[pl.ds(pl.multiple_of(a * R, R), R), :], buf.at[lax.rem(a, 4)], isem.at[lax.rem(a, 4)])

    def cout(a):
        return pltpu.make_async_copy(buf.at[lax.rem(a, 4)], dx_ref.at[pl.ds(pl.multiple_of(a * R, R), R), :], osem.at[lax.rem(a, 4)])

    @pl.when(g == 0)
    def _():
        cin(0).start()
        cin(1).start()
    for j in range(2):
        a = 2 * g + j
        cin(a).wait()
        cout(a).start()

        @pl.when(g > 0)
        def _():
            cout(a - 2).wait()

        @pl.when(g < ng - 1)
        def _():
            cin(a + 2).start()
    res = jnp.dot(og_ref[...], dy_ref[...], preferred_element_type=F32).astype(BF)
    gw_ref[...] = res[:d]
    gd_ref[...] = res[d:]
    gq_ref[...] = ot_ref[:C, :].T
    gu_ref[...] = ot_ref[C:, :].T

    @pl.when(g == ng - 1)
    def _():
        cout(2 * g).wait()
        cout(2 * g + 1).wait()


def finish(d, C, og, dy, ot, gathered, NB=512):
    M, T = og.shape
    D = dy.shape[1]
    CF = ot.shape[0]
    steps = D // NB
    R = T // (2 * steps)
    return pl.pallas_call(
        functools.partial(finish_kernel, d, C),
        grid=(steps,),
        in_specs=[pl.BlockSpec((M, T), lambda t: (0, 0), pipeline_mode=pl.Buffered(1)),
                  pl.BlockSpec((T, NB), lambda t: (0, t)),
                  pl.BlockSpec((CF, NB), lambda t: (0, t)),
                  pl.BlockSpec(memory_space=pl.ANY)],
        out_specs=[pl.BlockSpec((d, NB), lambda t: (0, t)), pl.BlockSpec((M - d, NB), lambda t: (0, t)),
                   pl.BlockSpec((NB, C), lambda t: (t, 0)), pl.BlockSpec((NB, CF - C), lambda t: (t, 0)),
                   pl.BlockSpec(memory_space=pl.ANY)],
        out_shape=[jax.ShapeDtypeStruct((d, D), BF), jax.ShapeDtypeStruct((M - d, D), BF),
                   jax.ShapeDtypeStruct((D, C), BF), jax.ShapeDtypeStruct((D, CF - C), BF),
                   jax.ShapeDtypeStruct((T, D), BF)],
        scratch_shapes=[pltpu.VMEM((4, R, D), BF), pltpu.SemaphoreType.DMA((4,)), pltpu.SemaphoreType.DMA((4,))],
        compiler_params=pltpu.CompilerParams(vmem_limit_bytes=VMEM_LIMIT),
        name="finish_grads",
    )(og, dy, ot, gathered)


def solution(mesh):
    row_spec = P('dp', None, None)
    in_specs = (row_spec, P(None), P(None), P(None, 'tp', None), P('tp', None), P(None, 'tp'), P('tp', None), row_spec)
    out_specs = (row_spec, P('dp', 'tp', None), P(('dp', 'tp'), None), P('dp', 'tp'), P(('dp', 'tp'), None))
    chips = mesh.shape['tp'] // CORES
    side = int(round(chips ** 0.5))
    assert side * side == chips

    def device_step(tokens, ln_gain, ln_bias, w_qkv, w_out, w_up, w_down, grad_out):
        rows, seq, D = tokens.shape
        T = rows * seq
        C = w_qkv.shape[1] * w_qkv.shape[2]
        d = w_out.shape[0]
        x = tokens.reshape(T, D)
        dy = grad_out.reshape(T, D)
        wt = jnp.concatenate([w_qkv.reshape(D, C).T, w_up.T], axis=0)
        wd = jnp.concatenate([w_out, w_down], axis=0)
        ln, dc, og, sh = forward('tp', side, x, dy, ln_gain, ln_bias, wt, wd, seq)
        ot, gathered = gather('tp', side, sh, dc, ln)
        gw, gd, gq, gu, dx = finish(d, C, og, dy, ot, gathered.reshape(T, D))
        return dx.reshape(tokens.shape), gq.reshape(w_qkv.shape), gw, gu, gd

    return jax.shard_map(device_step, mesh=mesh, in_specs=in_specs, out_specs=out_specs, check_vma=False)
```

time: 1360 us -> 632 us (0.46); the launches traced: 1340 us -> 632 us
  matrix products: 611 us -> 0 us
  Pallas kernels: 0 us -> 610 us
  other arithmetic: 338 us -> 11.4 us
  waiting for transfers between devices: 279 us -> 0 us
  local copies, waits for them, and re-layouts: 98.7 us -> 9.51 us
  between operations: 14.6 us -> 0.82 us
    dot_general x202 -> x0, matrix products: 611 us -> none  [the longest x1 72.4 us: branch_grads(): jnp.einsum('tf,hf->th', d_hidden, w_up, preferred_element_type=jnp.float32)]
    pallas_call x0 -> x3, Pallas kernels: none -> 610 us  [the longest x1 331 us: forward(): pl.pallas_call(functools.partial(forward_kernel, axis, side, S, d, C, F,...]
    psum x1 -> x0, waiting for transfers between devices: 279 us -> none  [device_step(): lax.psum(part_norm.astype(jnp.bfloat16), 'tp').astype(jnp.float32)]
    convert_element_type x3 -> x0, other arithmetic: 175 us -> none  [the longest x2 89.4 us: branch_grads(): normed = (x_hat * ln_gain + ln_bias).astype(jnp.bfloat16)]
    reduce_sum x35 -> x0, other arithmetic: 90.9 us -> none  [the longest x1 43.5 us: finish_norm(): jnp.mean(d_hat, axis=-1, keepdims=True)]
    dynamic_update_slice x32 -> x0, other arithmetic: 49 us -> none  [attend_rows(): return lax.map(one_row, (qkv_rows, dout_rows))]
    squeeze x32 -> x0, local copies, waits for them, and re-layouts: 30.1 us -> none  [attend_rows(): return lax.map(one_row, (qkv_rows, dout_rows))]
    dynamic_update_slice x64 -> x0, local copies, waits for them, and re-layouts: 24.3 us -> none  [attend_rows(): return lax.map(one_row, (qkv_rows, dout_rows))]
  transfers between devices with their start and end apart: 1 -> 0, of which waited for: 1 -> 0; matrix products, arithmetic and copies ran while one was open for 12% -> 0% of each run, Pallas kernels for 0% -> 0%
where the time goes in v1:
time: 632 us
  Pallas kernels  610 us (97%)
  other arithmetic  11.4 us (2%)
  local copies, waits for them, and re-layouts  9.51 us (2%)
    pallas_call x1, Pallas kernels, forward(): pl.pallas_call(functools.partial(forward_kernel, axis, side, S, d, C, F,...  331 us
    pallas_call x1, Pallas kernels, gather(): pl.pallas_call(functools.partial(gather_kernel, axis, side, NP), grid=(D...  192 us
    pallas_call x1, Pallas kernels, finish(): pl.pallas_call(functools.partial(finish_kernel, d, C), grid=(steps,), in_...  86.4 us

profile of v1, /device:TPU:97, one launch (start us, length us, event | category | flops | bytes accessed | tf_op | source)
XLA Modules:
  0.0 631.5 jit_solution(1114909107083369387)
XLA Ops:
  0.6 3.2 copy.13
  3.8 6.3 %copy.14 = bf16[4096,512]{0,1:T(8,128)(2,1)} copy(bf16[4096,512]{1,0:T(8,128)(2,1)} %param.13) | data formatting | bytes 8388608 | tf_op args[5]
  10.1 0.0 copy-start
  10.2 6.2 pad_maximum_fusion.wt_ref
  16.4 0.0 copy-done
  16.4 5.1 pad_maximum_fusion.1.wd_ref
  21.5 331.0 %forward_rs.1 = (bf16[8192,4096]{1,0:T(8,128)(2,1)}, bf16[896,8192]{1,0:T(8,128)(2,1)}, bf16[640,8192]{1,0:T(8,128)(2,1)}, bf16[16,16,4096]{2,1,0:T(8,128)(2,1)}) custom-call(bf16[8192,4096]{1,0:T(8,128)(2,1)} %bitcast.x0_ref.x_ref.xh_ref, bf16[8192,4096]{1,0:T(8,128)(2,1)} %bitcast.x0_ref.x_ref.xh_ref, bf16[8192,4096]{1,0:T(8,128)(2,1)} %bitcast.1.dy_ref.dyh_ref, ...), custom_call_target="tpu_custom_call" | custom-call | tf_op jit(solution)/shard_map/forward_rs/pallas_call | solution.py:319
  352.6 192.4 %gather_grads.1 = (bf16[896,4096]{1,0:T(8,128)(2,1)}, bf16[16,2,4,4,16,4096]{5,4,3,2,1,0:T(8,128)(2,1)}) custom-call(bf16[16,16,4096]{2,1,0:T(8,128)(2,1)} %get-tuple-element.17.sh_ref, bf16[896,8192]{1,0:T(8,128)(2,1)} %get-tuple-element.18.dc_ref, bf16[8192,4096]{1,0:T(8,128)(2,1)} %get-tuple-element.19.ln_ref), custom_call_target="tpu_custom_call" | custom-call | tf_op jit(solution)/shard_map/gather_grads/pallas_call | solution.py:455
  545.0 86.4 %finish_grads.1 = (bf16[128,4096]{1,0:T(8,128)(2,1)}, bf16[512,4096]{1,0:T(8,128)(2,1)}, bf16[4096,384]{1,0:T(8,128)(2,1)}, bf16[4096,512]{1,0:T(8,128)(2,1)}, bf16[8192,4096]{1,0:T(8,128)(2,1)}) custom-call(bf16[640,8192]{1,0:T(8,128)(2,1)} %get-tuple-element.16.og_ref, bf16[8192,4096]{1,0:T(8,128)(2,1)} %bitcast.1.dy_ref.dyh_ref, ...), custom_call_target="tpu_custom_call" | custom-call | tf_op jit(solution)/shard_map/finish_grads/pallas_call | solution.py:516
Async XLA Ops:
  10.1 6.2 copy-start

commit v2 on v1

v2 whole, which is shorter than its diff:
```python
import functools
import jax
import jax.numpy as jnp
from jax import lax
from jax.experimental import pallas as pl
from jax.experimental.pallas import tpu as pltpu
from jax.sharding import PartitionSpec as P

EPS = 1e-5
GELU_COEF = 0.7071067811865476
PDF_COEF = 0.3989422804014327
F32 = jnp.float32
BF = jnp.bfloat16
VMEM_LIMIT = 64 * 2**20 - 65536
CORES = 2
COLORS = 4
AG_EVERY = 24
NB = 512


def dg(a, b, ca, cb):
    return lax.dot_general(a, b, (((ca,), (cb,)), ((), ())), preferred_element_type=F32)


def normalize(x):
    x = x.astype(F32)
    c = x - jnp.mean(x, axis=-1, keepdims=True)
    r = lax.rsqrt(jnp.mean(c * c, axis=-1, keepdims=True) + EPS)
    return c * r, r


def ln_rows(x_ref, dst, rows, g_ref, b_ref, CH=512):
    D = x_ref.shape[1]
    tot = sq = None
    for c in range(0, D, CH):
        v = jnp.sum(x_ref[rows, c:c + CH].astype(F32), axis=-1, keepdims=True)
        tot = v if tot is None else tot + v
    mean = tot * (1.0 / D)
    for c in range(0, D, CH):
        v = x_ref[rows, c:c + CH].astype(F32) - mean
        v = jnp.sum(v * v, axis=-1, keepdims=True)
        sq = v if sq is None else sq + v
    r = lax.rsqrt(sq * (1.0 / D) + EPS)
    for c in range(0, D, CH):
        v = x_ref[rows, c:c + CH].astype(F32) - mean
        dst[rows, c:c + CH] = (v * r * g_ref[:, c:c + CH] + b_ref[:, c:c + CH]).astype(BF)


class Tile:
    def __init__(self, ln, dy, wt, wd, dct, qkv_s, do_s, h_s, da_s, og_ref, dc_ref, st_s, dp_s, p_b, ds_b, C, F, d, store):
        self.ln, self.dy, self.wt, self.wd, self.dct = ln, dy, wt, wd, dct
        self.qkv_s, self.do_s, self.h_s, self.da_s = qkv_s, do_s, h_s, da_s
        self.og_ref, self.dc_ref, self.st_s, self.dp_s, self.p_b, self.ds_b = og_ref, dc_ref, st_s, dp_s, p_b, ds_b
        self.C, self.F, self.d, self.store = C, F, d, store
        self.S, self.D = ln.shape

    def project(self, side, pieces):
        wt, wd, C, d, half = self.wt, self.wd, self.C, self.d, self.F // 2

        def more(j):
            for i in range(pieces * j // 5, pieces * (j + 1) // 5):
                side(i)
        self.qkv_s[...] = dg(wt[:C, :], self.ln[...], 1, 1).astype(BF)
        more(0)
        y = dg(wd[:d + half, :], self.dy[...], 1, 1)
        self.do_s[...] = y[:d].astype(BF)
        self.da_s[:half, :] = y[d:]
        more(1)
        self.h_s[:half, :] = dg(wt[C:C + half, :], self.ln[...], 1, 1)
        more(2)
        self.da_s[half:, :] = dg(wd[d + half:, :], self.dy[...], 1, 1)
        more(3)
        self.h_s[half:, :] = dg(wt[C + half:, :], self.ln[...], 1, 1)
        more(4)

    def col(self, i):
        self.store(i, dg(self.dct[...], self.wt[:, i * NB:(i + 1) * NB], 1, 0).astype(BF))

    def gelu(self, i, n):
        for j in range(2):
            r0 = (2 * i + j) * n
            h = self.h_s[r0:r0 + n, :]
            cdf = 0.5 * (1.0 + lax.erf(h * GELU_COEF))
            self.og_ref[self.d + r0:self.d + r0 + n, :] = (h * cdf).astype(BF)
            slope = cdf + h * PDF_COEF * jnp.exp(-0.5 * h * h)
            self.dc_ref[self.C + r0:self.C + r0 + n, :] = (self.da_s[r0:r0 + n, :] * slope).astype(BF)

    def softmax(self, scale, QC=128):
        S = self.S
        for c in range(0, S, QC):
            kk = c + QC
            qs = slice(c, c + QC)
            st = self.st_s[:kk, qs] * scale
            ki = lax.broadcasted_iota(jnp.int32, (kk, QC), 0)
            qi = lax.broadcasted_iota(jnp.int32, (kk, QC), 1) + c
            st = jnp.where(ki <= qi, st, -1e30)
            e = jnp.exp(st - jnp.max(st, axis=0, keepdims=True))
            p = e / jnp.sum(e, axis=0, keepdims=True)
            dp = self.dp_s[:kk, qs]
            rd = jnp.sum(p * dp, axis=0, keepdims=True)
            self.p_b[:kk, qs] = p.astype(BF)
            self.ds_b[:kk, qs] = (p * (dp - rd) * scale).astype(BF)
            if kk < S:
                self.p_b[kk:, qs] = jnp.zeros((S - kk, QC), BF)
                self.ds_b[kk:, qs] = jnp.zeros((S - kk, QC), BF)

    def rest(self):
        d = self.d
        scale = d ** -0.5
        n = self.D // NB
        rows = self.F // (2 * n)
        q, k, v, do = self.qkv_s[:d, :], self.qkv_s[d:2 * d, :], self.qkv_s[2 * d:3 * d, :], self.do_s[...]
        self.col(0)
        self.st_s[...] = dg(k, q, 0, 0)
        self.dp_s[...] = dg(v, do, 0, 0)
        self.col(1)
        self.gelu(0, rows)
        self.gelu(1, rows)
        self.softmax(scale)
        self.col(2)
        self.gelu(2, rows)
        self.og_ref[:d, :] = dg(v, self.p_b[...], 1, 0).astype(BF)
        self.dc_ref[2 * d:3 * d, :] = dg(do, self.p_b[...], 1, 1).astype(BF)
        self.col(3)
        self.gelu(3, rows)
        self.dc_ref[:d, :] = dg(k, self.ds_b[...], 1, 0).astype(BF)
        self.dc_ref[d:2 * d, :] = dg(q, self.ds_b[...], 1, 1).astype(BF)
        for i in range(4, n):
            self.col(i)
            self.gelu(i, rows)
        self.dct[...] = self.dc_ref[...].T

    def last(self):
        for i in range(self.D // NB):
            self.col(i)


class Place:
    def __init__(self, axis, side):
        self.axis, self.side = axis, side
        i = lax.axis_index(axis)
        self.c = lax.rem(i, CORES)
        chip = lax.div(i, CORES)
        x, y = lax.rem(chip, side), lax.div(chip, side)
        self.at = {"x": [x] + [lax.rem(x + j, side) for j in range(1, side)],
                   "y": [y] + [lax.rem(y + j, side) for j in range(1, side)]}
        self.x, self.y = x, y
        self.next = {}
        for sg in (1, -1):
            self.next["x", sg] = self.index(self.block("x", sg), y, self.c)
            self.next["y", sg] = self.index(x, self.block("y", sg), self.c)
        self.other = self.index(x, y, 1 - self.c)

    def index(self, x, y, c):
        return (y * self.side + x) * CORES + c

    def step(self, along, by):
        return self.next[along, by]

    def peer(self):
        return self.other

    def block(self, along, by):
        return self.at[along][by % self.side]

    def partners(self):
        return [self.step("x", 1), self.step("x", -1), self.step("y", 1), self.step("y", -1), self.peer()]

    def greet(self):
        sem = pltpu.get_barrier_semaphore()
        who = self.partners()
        for w in who:
            pl.semaphore_signal(sem, inc=1, device_id={self.axis: w}, device_id_type=pl.DeviceIdType.MESH)
        pl.semaphore_wait(sem, len(who))


RINGS = (("x", "y", 1), ("x", "y", -1), ("y", "x", 1), ("y", "x", -1))


class Gather:
    def __init__(self, me, g_ref, own, base, PU, snd, rcv, p_snd, p_rcv, own_sem):
        self.me, self.g, self.own, self.base, self.PU = me, g_ref, own, base, PU
        self.snd, self.rcv, self.p_snd, self.p_rcv, self.own_sem = snd, rcv, p_snd, p_rcv, own_sem
        self.HA = me.side - 1
        self.CW = g_ref.shape[-1] // COLORS

    def send(self, src, dst, ssem, rsem, dev):
        return pltpu.make_async_remote_copy(src_ref=src, dst_ref=dst, send_sem=ssem, recv_sem=rsem,
                                            device_id={self.me.axis: dev}, device_id_type=pl.DeviceIdType.MESH)

    def units(self, p):
        return pl.ds(self.base + p * self.PU, self.PU)

    def region(self, p, k, h, lag):
        me = self.me
        along_b, along_a, sg = RINGS[k]
        cw = pl.ds(k * self.CW, self.CW)
        if h < self.HA:
            b = me.block(along_a, -sg * lag)
            xi, yi = (me.x, b) if along_a == "y" else (b, me.y)
            return self.g.at[self.units(p), me.c, xi, yi, :, cw]
        b = me.block(along_b, -sg * lag)
        if along_b == "x":
            return self.g.at[self.units(p), me.c, b, :, :, cw]
        return self.g.at[self.units(p), me.c, :, b, :, cw]

    def hop(self, p, k, h):
        along_b, along_a, sg = RINGS[k]
        dst = self.region(p, k, h, h if h < self.HA else h - self.HA)
        src = self.own.at[pl.ds(p * self.PU, self.PU), :, pl.ds(k * self.CW, self.CW)] if h == 0 else dst
        return self.send(src, dst, self.snd.at[p, k, h], self.rcv.at[p, k, h],
                         self.me.step(along_a if h < self.HA else along_b, sg))

    def mine(self, p):
        return self.g.at[self.units(p), self.me.c, self.me.x, self.me.y]

    def keep(self, p):
        return pltpu.make_async_copy(self.own.at[pl.ds(p * self.PU, self.PU)], self.mine(p), self.own_sem.at[p])

    def to_peer(self, src, dst):
        return self.send(src, dst, self.p_snd, self.p_rcv, self.me.peer())

    def begin(self, p):
        for k in range(COLORS):
            self.hop(p, k, 0).start()
        self.keep(p).start()
        self.to_peer(self.own.at[pl.ds(p * self.PU, self.PU)], self.mine(p)).start()

    def arrived(self, p, h):
        HA = self.HA
        if h == HA - 1:
            self.keep(p).wait()
        for k in range(COLORS):
            self.hop(p, k, h).wait()
            if h < 2 * HA - 1:
                self.hop(p, k, h + 1).start()
            got = self.region(p, k, h, (h if h < HA else h - HA) + 1)
            self.to_peer(got, got).start()

    def end(self, count):
        every = self.g.at[pl.ds(self.base, count * self.PU), self.me.c]
        self.to_peer(every, every).wait()


def forward_kernel(axis, side, S, d, C, F, nt, PU, early,
                   x0_ref, x_ref, dy_ref, g_ref, b_ref, wqh_ref, wuh_ref, woh_ref, wdh_ref, xh_ref, dyh_ref,
                   lnh_ref, dc_ref, og_ref, sh_ref, gat_ref,
                   wt_ref, wd_ref, wq_s, wu_s, ln_s, h_s, da_s, qkv_s, do_s, dct_s, st_s, dp_s, p_b, ds_b, p_s, q_s, r1_s, r2_s, fx_s, fd_s, fo_s,
                   w_sem, wst_sem, ln_sem, s0_send, s0_recv, s1_send, s1_recv, s2_send, s2_recv, f_sem, fo_sem,
                   a_send, a_recv, ap_send, ap_recv, ao_sem):
    TM, D = x_ref.shape
    n = side
    me = Place(axis, side)
    g = pl.program_id(0)
    slot = lax.rem(g, 2)
    nxt = 1 - slot
    nu = nt // 2
    CW = D // COLORS
    QB = q_s.shape[0]
    RB = r1_s.shape[0]
    RR = q_s.shape[3]

    def copy_to(src, dst, ssem, rsem, dev):
        return pltpu.make_async_remote_copy(src_ref=src, dst_ref=dst, send_sem=ssem, recv_sem=rsem,
                                            device_id={axis: dev}, device_id_type=pl.DeviceIdType.MESH)

    def cols(k):
        return pl.ds(k * CW, CW)

    def st0(u):
        return copy_to(p_s.at[lax.rem(u, 2), 1 - me.c], q_s.at[lax.rem(u, QB)], s0_send.at[lax.rem(u, QB)], s0_recv.at[lax.rem(u, QB)], me.peer())

    def q_block(u, k, by):
        along = RINGS[k][0]
        q = q_s.at[lax.rem(u, QB)]
        b = me.block(along, by)
        return q.at[b, :, :, cols(k)] if along == "x" else q.at[:, b, :, cols(k)]

    def st1(u, k, s):
        along, _, sg = RINGS[k]
        rs = lax.rem(u, RB)
        src = q_block(u, k, -sg) if s == 0 else r1_s.at[rs, s - 1, k]
        return copy_to(src, r1_s.at[rs, s, k], s1_send.at[rs, s, k], s1_recv.at[rs, s, k], me.step(along, sg))

    def st2(u, k, s):
        _, along, sg = RINGS[k]
        rs = lax.rem(u, RB)
        src = r1_s.at[rs, n - 2, k, me.block(along, -sg)] if s == 0 else r2_s.at[rs, s - 1, k]
        return copy_to(src, r2_s.at[rs, s, k], s2_send.at[rs, s, k], s2_recv.at[rs, s, k], me.step(along, sg))

    def on_st0(u):
        st0(u).wait()
        qi, pi = lax.rem(u, QB), lax.rem(u, 2)

        for a in range(n):
            for b in range(n):
                q_s[qi, a, b] = q_s[qi, a, b] + p_s[pi, me.c, a, b]
        for k in range(COLORS):
            st1(u, k, 0).start()

    def on_st1(u, s):
        for k in range(COLORS):
            st1(u, k, s).wait()
        rs = lax.rem(u, RB)
        for k in range(COLORS):
            sg = RINGS[k][2]
            own = q_block(u, k, -sg * (2 + s))

            r1_s[rs, s, k] = r1_s[rs, s, k] + own[...]
        for k in range(COLORS):
            (st1(u, k, s + 1) if s < n - 2 else st2(u, k, 0)).start()

    def shard_rows(u):
        r = u * 2 * TM + ((me.c * n + me.x) * n + me.y) * RR
        return pl.ds(pl.multiple_of(r, RR), RR)

    def fetch(u):
        return (pltpu.make_async_copy(xh_ref.at[shard_rows(u), :], fx_s, f_sem.at[0]),
                pltpu.make_async_copy(dyh_ref.at[shard_rows(u), :], fd_s, f_sem.at[1]))

    UE = early * PU
    ag = Gather(me, gat_ref, fo_s, 0, PU, a_send, a_recv, ap_send, ap_recv, ao_sem)

    def put(u):
        return pltpu.make_async_copy(fo_s.at[UE + lax.rem(u, 2)], sh_ref.at[u - UE], fo_sem.at[lax.rem(u, 2)])

    def on_st2(u, s):
        for k in range(COLORS):
            st2(u, k, s).wait()
        rs = lax.rem(u, RB)
        for k in range(COLORS):
            along, sg = RINGS[k][1], RINGS[k][2]
            own = r1_s.at[rs, n - 2, k, me.block(along, -sg * (2 + s))]
            r2_s[rs, s, k] = r2_s[rs, s, k] + own[...]
            if s < n - 2:
                st2(u, k, s + 1).start()
        if s == n - 3:
            for f in fetch(u):
                f.start()
        if s == n - 2:
            for f in fetch(u):
                f.wait()

            xhat, r = normalize(fx_s[...])
            total = jnp.concatenate([r2_s[rs, s, k] for k in range(COLORS)], axis=-1).astype(F32)
            dh = total * g_ref[...]
            gx = r * (dh - jnp.mean(dh, axis=-1, keepdims=True) - xhat * jnp.mean(dh * xhat, axis=-1, keepdims=True))
            done = (fd_s[...].astype(F32) + gx).astype(BF)

            @pl.when(u < UE)
            def _():
                fo_s[u] = done

            @pl.when((u < UE) & (lax.rem(u, PU) == PU - 1))
            def _():
                ag.begin(lax.div(u, PU))

            @pl.when(u >= UE + 2)
            def _():
                put(u - 2).wait()

            @pl.when(u >= UE)
            def _():
                fo_s[UE + lax.rem(u, 2)] = done
                put(u).start()

            @pl.when(u == nu - 1)
            def _():
                put(u - 1).wait()
                put(u).wait()

    rs_at = (4, 10, 16, 22, 26, 30, 34)
    ag_at = (6, 10, 14, 22, 30, 38)
    steps = [on_st0] + [functools.partial(on_st1, s=s) for s in range(n - 1)] + [functools.partial(on_st2, s=s) for s in range(n - 1)]

    def comm(r):
        now = 4 * g + r
        for rho, fn in reversed(list(zip(rs_at, steps, strict=True))):
            if rho % 4 != r:
                continue
            back = 3 + rho // 4
            u = lax.div(g - back, 2)

            @pl.when((g >= back) & (lax.rem(g - back + 2 * nt, 2) == 0) & (u < nu))
            def _():
                fn(u)
        for h, o in enumerate(ag_at):
            first = 8 * (PU - 1) + 12 + rs_at[-1] + o
            if first % 4 != r:
                continue
            p = lax.div(now - first, AG_EVERY)

            @pl.when((now >= first) & (lax.rem(now - first + 64 * AG_EVERY, AG_EVERY) == 0) & (p < early))
            def _():
                ag.arrived(p, h)

    def out_copy(sl, tt):
        return pltpu.make_async_copy(ln_s.at[sl], lnh_ref.at[pl.ds(pl.multiple_of(tt * TM, TM), TM), :], ln_sem.at[sl])

    @pl.when(g == 0)
    def _():
        WR = wq_s.shape[1]

        def w_in(i):
            rows = pl.ds(pl.multiple_of(i * WR, WR), WR)
            j = lax.rem(i, 2)
            return (pltpu.make_async_copy(wqh_ref.at[rows, :], wq_s.at[j], wst_sem.at[j, 0]),
                    pltpu.make_async_copy(wuh_ref.at[rows, :], wu_s.at[j], wst_sem.at[j, 1]))
        whole = (pltpu.make_async_copy(woh_ref, wd_ref.at[pl.ds(0, d), :], w_sem.at[0]),
                 pltpu.make_async_copy(wdh_ref, wd_ref.at[pl.ds(d, F), :], w_sem.at[1]))
        for cp in w_in(0) + w_in(1) + whole:
            cp.start()
        me.greet()

        dct_s[...] = jnp.zeros_like(dct_s)

        def lnb(i, _):
            ln_rows(x0_ref, ln_s.at[0], pl.ds(pl.multiple_of(i * 16, 16), 16), g_ref, b_ref)
            return 0
        lax.fori_loop(0, TM // 16, lnb, 0)

        def wtb(i, _):
            for cp in w_in(i):
                cp.wait()
            to = pl.ds(pl.multiple_of(i * WR, WR), WR)
            j = lax.rem(i, 2)
            wt_ref[:C, to] = wq_s[j].T
            wt_ref[C:, to] = wu_s[j].T

            @pl.when(i + 2 < D // WR)
            def _():
                for cp in w_in(i + 2):
                    cp.start()
            return 0
        lax.fori_loop(0, D // WR, wtb, 0)
        for cp in whole:
            cp.wait()

    live = g < nt

    @pl.when((g > 0) & (g <= nt))
    def _():
        out_copy(nxt, g - 1).wait()

    before = g + 3

    def store(i, v):
        p_s[lax.rem(lax.div(before, 2), 2), lax.rem(before, 2), :, :, :, pl.ds(i * NB, NB)] = v.reshape(n, n, RR, NB)
    tile = Tile(ln_s.at[slot], dy_ref, wt_ref, wd_ref, dct_s, qkv_s, do_s, h_s, da_s,
                og_ref, dc_ref, st_s, dp_s, p_b, ds_b, C, F, d, store)

    comm(0)

    @pl.when(live)
    def _():
        out_copy(slot, g).start()
        tile.project(lambda i: ln_rows(x_ref, ln_s.at[nxt], pl.ds(i * 8, 8), g_ref, b_ref), TM // 8)

    comm(2)

    @pl.when(live)
    def _():
        tile.rest()

    @pl.when(g == nt)
    def _():
        tile.last()

    @pl.when((g > 0) & (g <= nt) & (slot == 0))
    def _():
        st0(lax.div(g, 2) - 1).start()

    @pl.when(g == pl.num_programs(0) - 1)
    def _():
        ag.end(early)


def forward(axis, side, x, dy, gain, bias, w_qkv, w_up, w_out, w_down, S, TM=256, PU=2, early=2):
    T, D = x.shape
    C, F, d = w_qkv.shape[1], w_up.shape[1], w_out.shape[0]
    CF, dF = C + F, d + F
    nt = T // TM
    nu = nt // 2
    RR = 2 * TM // (CORES * side * side)
    drain = 10
    CW = D // COLORS
    last = nt - 1
    QB, RB, WR = 4, 5, 512
    UE = early * PU
    hops = 2 * (side - 1)
    dma = pltpu.SemaphoreType.DMA
    anyspace = pl.BlockSpec(memory_space=pl.ANY)
    return pl.pallas_call(
        functools.partial(forward_kernel, axis, side, S, d, C, F, nt, PU, early),
        grid=(nt + drain,),
        in_specs=[pl.BlockSpec((TM, D), lambda t: (0, 0), pipeline_mode=pl.Buffered(1)),
                  pl.BlockSpec((TM, D), lambda t: (jnp.minimum(t + 1, last), 0)),
                  pl.BlockSpec((TM, D), lambda t: (jnp.minimum(t, last), 0)),
                  pl.BlockSpec((1, D), lambda t: (0, 0)),
                  pl.BlockSpec((1, D), lambda t: (0, 0))] + [anyspace] * 6,
        out_specs=[anyspace,
                   pl.BlockSpec((CF, TM), lambda t: (0, jnp.minimum(t, last))),
                   pl.BlockSpec((dF, TM), lambda t: (0, jnp.minimum(t, last))),
                   anyspace, anyspace],
        out_shape=[jax.ShapeDtypeStruct((T, D), BF), jax.ShapeDtypeStruct((CF, T), BF),
                   jax.ShapeDtypeStruct((dF, T), BF), jax.ShapeDtypeStruct((nu - UE, RR, D), BF),
                   jax.ShapeDtypeStruct((nu, CORES, side, side, RR, D), BF)],
        scratch_shapes=[pltpu.VMEM((CF, D), BF), pltpu.VMEM((dF, D), BF),
                        pltpu.VMEM((2, WR, C), BF), pltpu.VMEM((2, WR, F), BF),
                        pltpu.VMEM((2, TM, D), BF), pltpu.VMEM((F, TM), F32), pltpu.VMEM((F, TM), F32),
                        pltpu.VMEM((C, TM), BF), pltpu.VMEM((d, TM), BF), pltpu.VMEM((TM, CF), BF),
                        pltpu.VMEM((S, S), F32), pltpu.VMEM((S, S), F32), pltpu.VMEM((S, S), BF), pltpu.VMEM((S, S), BF),
                        pltpu.VMEM((2, CORES, side, side, RR, D), BF),
                        pltpu.VMEM((QB, side, side, RR, D), BF),
                        pltpu.VMEM((RB, side - 1, COLORS, side, RR, CW), BF),
                        pltpu.VMEM((RB, side - 1, COLORS, RR, CW), BF),
                        pltpu.VMEM((RR, D), BF), pltpu.VMEM((RR, D), BF), pltpu.VMEM((UE + 2, RR, D), BF),
                        dma((2,)), dma((2, 2)), dma((2,)), dma((QB,)), dma((QB,)),
                        dma((RB, side - 1, COLORS)), dma((RB, side - 1, COLORS)),
                        dma((RB, side - 1, COLORS)), dma((RB, side - 1, COLORS)),
                        dma((2,)), dma((2,)),
                        dma((early, COLORS, hops)), dma((early, COLORS, hops)), dma, dma, dma((early,))],
        compiler_params=pltpu.CompilerParams(vmem_limit_bytes=VMEM_LIMIT, collective_id=1, has_side_effects=True),
        name="forward_rs",
    )(x, x, dy, gain.reshape(1, D), bias.reshape(1, D), w_qkv, w_up, w_out, w_down, x, dy)


def gather_kernel(axis, side, base, PU, sh_ref, dc_ref, og_ref, ln_ref, dy_ref, gin_ref, o1_ref, o2_ref, g_ref,
                  own_s, dc_s, og_s, l_sem, dc_sem, og_sem, snd, rcv, p_snd, p_rcv, own_sem):
    me = Place(axis, side)
    g = pl.program_id(0)
    ng = pl.num_programs(0)
    nl = sh_ref.shape[0]
    NP = nl // PU
    HA = side - 1
    M1, M2 = dc_s.shape[0] // 2, og_s.shape[0] // 2
    ag = Gather(me, g_ref, own_s, base, PU, snd, rcv, p_snd, p_rcv, own_sem)

    def left(j):
        src, dst, sem, M = ((dc_ref, dc_s, dc_sem, M1), (og_ref, og_s, og_sem, M2))[j // 2]
        rows = pl.ds((j % 2) * M, M)
        return pltpu.make_async_copy(src.at[rows, :], dst.at[rows, :], sem.at[j % 2])

    @pl.when(g == 0)
    def _():
        ld = pltpu.make_async_copy(sh_ref, own_s, l_sem)
        ld.start()
        left(0).start()
        me.greet()
        ld.wait()
        for p in range(NP):
            ag.begin(p)
        left(1).start()
        left(2).start()
        left(3).start()

    for j in range(2):
        @pl.when(g == 0)
        def _():
            left(2 * j).wait()
            left(2 * j + 1).wait()
        src, rhs, o_ref, M = ((dc_s, ln_ref, o1_ref, M1), (og_s, dy_ref, o2_ref, M2))[j]
        for i in range(2):
            rows = pl.ds(i * M, M)
            o_ref[rows, :] = jnp.dot(src[rows, :], rhs[...], preferred_element_type=F32).astype(BF)
        now = 2 * g + j
        half = -(-NP // 2)
        for h in range(HA):
            for i in range(half):
                p = lax.rem(now, 2) * half + i

                @pl.when((lax.div(now, 2) == h) & (p < NP))
                def _():
                    ag.arrived(p, h)
        left_rounds = 2 * ng - 2 * HA - 1
        many = HA * NP
        e = (now - 2 * HA - 1) * many
        for h in range(HA, 2 * HA):
            p = lax.div(e, left_rounds) - (h - HA) * NP

            @pl.when((e >= 0) & (lax.rem(e, left_rounds) < many) & (p >= 0) & (p < NP))
            def _():
                ag.arrived(p, h)

    @pl.when(g == ng - 1)
    def _():
        ag.end(NP)


def gather(axis, side, sh, dc, og, ln, dy, gathered, PU=2, NB=256):
    nl, RR, D = sh.shape
    nu = gathered.shape[0]
    CF, T = dc.shape
    dF = og.shape[0]
    NP = nl // PU
    hops = 2 * (side - 1)
    dma = pltpu.SemaphoreType.DMA
    anyspace = pl.BlockSpec(memory_space=pl.ANY)
    return pl.pallas_call(
        functools.partial(gather_kernel, axis, side, nu - nl, PU),
        grid=(D // NB,),
        in_specs=[anyspace] * 3 + [pl.BlockSpec((T, NB), lambda t: (0, t))] * 2 + [anyspace],
        out_specs=[pl.BlockSpec((CF, NB), lambda t: (0, t)), pl.BlockSpec((dF, NB), lambda t: (0, t)), anyspace],
        out_shape=[jax.ShapeDtypeStruct((CF, D), BF), jax.ShapeDtypeStruct((dF, D), BF),
                   jax.ShapeDtypeStruct(gathered.shape, BF)],
        scratch_shapes=[pltpu.VMEM((nl, RR, D), BF), pltpu.VMEM((CF, T), BF), pltpu.VMEM((dF, T), BF),
                        dma, dma((2,)), dma((2,)),
                        dma((NP, COLORS, hops)), dma((NP, COLORS, hops)), dma, dma, dma((NP,))],
        input_output_aliases={5: 2},
        compiler_params=pltpu.CompilerParams(vmem_limit_bytes=VMEM_LIMIT, collective_id=2, has_side_effects=True),
        name="gather_grads",
    )(sh, dc, og, ln, dy, gathered)


def finish_kernel(d, C, o1_ref, o2_ref, gh_ref, gw_ref, gd_ref, gq_ref, gu_ref, dx_ref, buf, isem, osem):
    g = pl.program_id(0)
    ng = pl.num_programs(0)
    R = buf.shape[1]

    def cin(a):
        return pltpu.make_async_copy(gh_ref.at[pl.ds(pl.multiple_of(a * R, R), R), :], buf.at[lax.rem(a, 4)], isem.at[lax.rem(a, 4)])

    def cout(a):
        return pltpu.make_async_copy(buf.at[lax.rem(a, 4)], dx_ref.at[pl.ds(pl.multiple_of(a * R, R), R), :], osem.at[lax.rem(a, 4)])

    @pl.when(g == 0)
    def _():
        cin(0).start()
        cin(1).start()
    for j in range(2):
        a = 2 * g + j
        cin(a).wait()
        cout(a).start()

        @pl.when(g > 0)
        def _():
            cout(a - 2).wait()

        @pl.when(g < ng - 1)
        def _():
            cin(a + 2).start()
    gw_ref[...] = o2_ref[:d, :]
    gd_ref[...] = o2_ref[d:, :]
    gq_ref[...] = o1_ref[:C, :].T
    gu_ref[...] = o1_ref[C:, :].T

    @pl.when(g == ng - 1)
    def _():
        cout(2 * g).wait()
        cout(2 * g + 1).wait()


def finish(d, C, o1, o2, gathered, NB=512):
    T, D = gathered.shape
    CF, dF = o1.shape[0], o2.shape[0]
    steps = D // NB
    R = T // (2 * steps)
    return pl.pallas_call(
        functools.partial(finish_kernel, d, C),
        grid=(steps,),
        in_specs=[pl.BlockSpec((CF, NB), lambda t: (0, t)),
                  pl.BlockSpec((dF, NB), lambda t: (0, t)),
                  pl.BlockSpec(memory_space=pl.ANY)],
        out_specs=[pl.BlockSpec((d, NB), lambda t: (0, t)), pl.BlockSpec((dF - d, NB), lambda t: (0, t)),
                   pl.BlockSpec((NB, C), lambda t: (t, 0)), pl.BlockSpec((NB, CF - C), lambda t: (t, 0)),
                   pl.BlockSpec(memory_space=pl.ANY)],
        out_shape=[jax.ShapeDtypeStruct((d, D), BF), jax.ShapeDtypeStruct((dF - d, D), BF),
                   jax.ShapeDtypeStruct((D, C), BF), jax.ShapeDtypeStruct((D, CF - C), BF),
                   jax.ShapeDtypeStruct((T, D), BF)],
        scratch_shapes=[pltpu.VMEM((4, R, D), BF), pltpu.SemaphoreType.DMA((4,)), pltpu.SemaphoreType.DMA((4,))],
        compiler_params=pltpu.CompilerParams(vmem_limit_bytes=VMEM_LIMIT),
        name="finish_grads",
    )(o1, o2, gathered)


def solution(mesh):
    row_spec = P('dp', None, None)
    in_specs = (row_spec, P(None), P(None), P(None, 'tp', None), P('tp', None), P(None, 'tp'), P('tp', None), row_spec)
    out_specs = (row_spec, P('dp', 'tp', None), P(('dp', 'tp'), None), P('dp', 'tp'), P(('dp', 'tp'), None))
    chips = mesh.shape['tp'] // CORES
    side = int(round(chips ** 0.5))
    assert side * side == chips

    def device_step(tokens, ln_gain, ln_bias, w_qkv, w_out, w_up, w_down, grad_out):
        rows, seq, D = tokens.shape
        T = rows * seq
        C = w_qkv.shape[1] * w_qkv.shape[2]
        d = w_out.shape[0]
        x = tokens.reshape(T, D)
        dy = grad_out.reshape(T, D)
        ln, dc, og, sh, gathered = forward('tp', side, x, dy, ln_gain, ln_bias, w_qkv.reshape(D, C), w_up, w_out, w_down, seq)
        o1, o2, gathered = gather('tp', side, sh, dc, og, ln, dy, gathered)
        gw, gd, gq, gu, dx = finish(d, C, o1, o2, gathered.reshape(T, D))
        return dx.reshape(tokens.shape), gq.reshape(w_qkv.shape), gw, gu, gd

    return jax.shard_map(device_step, mesh=mesh, in_specs=in_specs, out_specs=out_specs, check_vma=False)
```

time: 632 us -> 520 us (0.82)
  Pallas kernels: 610 us -> 519 us
  other arithmetic: 11.4 us -> 0 us
  local copies, waits for them, and re-layouts: 9.51 us -> 0 us
    pallas_call x1, Pallas kernels: 192 us -> 148 us  [gather(): pl.pallas_call(functools.partial(gather_kernel, axis, side, nu - nl, PU),...]
    pallas_call x1, Pallas kernels: 86.4 us -> 52.1 us  [finish(): pl.pallas_call(functools.partial(finish_kernel, d, C), grid=(steps,), in_...]
    concatenate x2 -> x0, other arithmetic: 11.4 us -> none  [the longest x1 6.24 us: device_step(): wt = jnp.concatenate([w_qkv.reshape(D, C).T, w_up.T], axis=0)]
    pallas_call x1, Pallas kernels: 331 us -> 320 us  [forward(): pl.pallas_call(functools.partial(forward_kernel, axis, side, S, d, C, F,...]
    unnamed x4 -> x0, local copies, waits for them, and re-layouts: 9.51 us -> none
where the time goes in v2:
time: 520 us
  Pallas kernels  519 us (100%)
    pallas_call x1, Pallas kernels, forward(): pl.pallas_call(functools.partial(forward_kernel, axis, side, S, d, C, F,...  320 us
    pallas_call x1, Pallas kernels, gather(): pl.pallas_call(functools.partial(gather_kernel, axis, side, nu - nl, PU),...  148 us
    pallas_call x1, Pallas kernels, finish(): pl.pallas_call(functools.partial(finish_kernel, d, C), grid=(steps,), in_...  52.1 us

profile of v2, /device:TPU:97, one launch (start us, length us, event | category | flops | bytes accessed | tf_op | source)
XLA Modules:
  0.0 520.3 jit_solution(8520424180694395072)
XLA Ops:
  0.6 319.8 %forward_rs.1 = (bf16[8192,4096]{1,0:T(8,128)(2,1)}, bf16[896,8192]{1,0:T(8,128)(2,1)}, bf16[640,8192]{1,0:T(8,128)(2,1)}, bf16[12,16,4096]{2,1,0:T(8,128)(2,1)}, bf16[16,2,4,4,16,4096]{5,4,3,2,1,0:T(8,128)(2,1)}) custom-call(bf16[8192,4096]{1,0:T(8,128)(2,1)} %bitcast.x0_ref.x_ref.xh_ref, bf16[8192,4096]{1,0:T(8,128)(2,1)} %bitcast.x0_ref.x_ref.xh_ref, ...), custom_call_target="tpu_custom_call" | custom-call | tf_op jit(solution)/shard_map/forward_rs/pallas_call | solution.py:493
  320.4 147.6 %gather_grads.1 = (bf16[896,4096]{1,0:T(8,128)(2,1)}, bf16[640,4096]{1,0:T(8,128)(2,1)}, bf16[16,2,4,4,16,4096]{5,4,3,2,1,0:T(8,128)(2,1)}) custom-call(bf16[12,16,4096]{2,1,0:T(8,128)(2,1)} %get-tuple-element.18.sh_ref, bf16[896,8192]{1,0:T(8,128)(2,1)} %get-tuple-element.19.dc_ref, ...), custom_call_target="tpu_custom_call", output_to_operand_aliasing={{2}: (5, {})} | custom-call | tf_op jit(solution)/shard_map/gather_grads/pallas_call | solution.py:599
  468.0 52.1 %finish_grads.1 = (bf16[128,4096]{1,0:T(8,128)(2,1)}, bf16[512,4096]{1,0:T(8,128)(2,1)}, bf16[4096,384]{1,0:T(8,128)(2,1)}, bf16[4096,512]{1,0:T(8,128)(2,1)}, bf16[8192,4096]{1,0:T(8,128)(2,1)}) custom-call(bf16[896,4096]{1,0:T(8,128)(2,1)} %get-tuple-element.23.o1_ref, bf16[640,4096]{1,0:T(8,128)(2,1)} %get-tuple-element.24.o2_ref, ...), custom_call_target="tpu_custom_call" | custom-call | tf_op jit(solution)/shard_map/finish_grads/pallas_call | solution.py:658

commit v3 on v2

--- a/solution.py
+++ b/solution.py
@@ -14,7 +14,7 @@
 VMEM_LIMIT = 64 * 2**20 - 65536
 CORES = 2
 COLORS = 4
-AG_EVERY = 24
+AG_EVERY = 32
 NB = 512
 
 
@@ -242,23 +242,23 @@
         self.to_peer(every, every).wait()
 
 
-def forward_kernel(axis, side, S, d, C, F, nt, PU, early,
-                   x0_ref, x_ref, dy_ref, g_ref, b_ref, wqh_ref, wuh_ref, woh_ref, wdh_ref, xh_ref, dyh_ref,
-                   lnh_ref, dc_ref, og_ref, sh_ref, gat_ref,
-                   wt_ref, wd_ref, wq_s, wu_s, ln_s, h_s, da_s, qkv_s, do_s, dct_s, st_s, dp_s, p_b, ds_b, p_s, q_s, r1_s, r2_s, fx_s, fd_s, fo_s,
-                   w_sem, wst_sem, ln_sem, s0_send, s0_recv, s1_send, s1_recv, s2_send, s2_recv, f_sem, fo_sem,
-                   a_send, a_recv, ap_send, ap_recv, ao_sem):
-    TM, D = x_ref.shape
+def layer_kernel(axis, side, S, TM, C, F, d, PU, early,
+                 x_ref, dy_ref, g_ref, b_ref, wqh_ref, wuh_ref, woh_ref, wdh_ref,
+                 lnh_ref, dch_ref, ogh_ref, gat_ref, o1h_ref, o2h_ref,
+                 q_s, r1_s, r2_s, fx_s, fd_s, fo_s,
+                 w_sem, wst_sem, x_sem, dy_sem, ln_sem, dc_sem, og_sem, s0_send, s0_recv, s1_send, s1_recv, s2_send, s2_recv,
+                 f_sem, a_send, a_recv, ap_send, ap_recv, ao_sem, l_sem, b_sem, o_sem):
+    T, D = x_ref.shape
     n = side
     me = Place(axis, side)
-    g = pl.program_id(0)
-    slot = lax.rem(g, 2)
-    nxt = 1 - slot
+    nt = T // TM
     nu = nt // 2
+    CF, dF = C + F, d + F
     CW = D // COLORS
     QB = q_s.shape[0]
     RB = r1_s.shape[0]
     RR = q_s.shape[3]
+    first_steps = nt + 3
 
     def copy_to(src, dst, ssem, rsem, dev):
         return pltpu.make_async_remote_copy(src_ref=src, dst_ref=dst, send_sem=ssem, recv_sem=rsem,
@@ -267,8 +267,8 @@
     def cols(k):
         return pl.ds(k * CW, CW)
 
-    def st0(u):
-        return copy_to(p_s.at[lax.rem(u, 2), 1 - me.c], q_s.at[lax.rem(u, QB)], s0_send.at[lax.rem(u, QB)], s0_recv.at[lax.rem(u, QB)], me.peer())
+    def tile_rows(t):
+        return pl.ds(pl.multiple_of(t * TM, TM), TM)
 
     def q_block(u, k, by):
         along = RINGS[k][0]
@@ -287,16 +287,6 @@
         rs = lax.rem(u, RB)
         src = r1_s.at[rs, n - 2, k, me.block(along, -sg)] if s == 0 else r2_s.at[rs, s - 1, k]
         return copy_to(src, r2_s.at[rs, s, k], s2_send.at[rs, s, k], s2_recv.at[rs, s, k], me.step(along, sg))
-
-    def on_st0(u):
-        st0(u).wait()
-        qi, pi = lax.rem(u, QB), lax.rem(u, 2)
-
-        for a in range(n):
-            for b in range(n):
-                q_s[qi, a, b] = q_s[qi, a, b] + p_s[pi, me.c, a, b]
-        for k in range(COLORS):
-            st1(u, k, 0).start()
 
     def on_st1(u, s):
         for k in range(COLORS):
@@ -305,7 +295,6 @@
         for k in range(COLORS):
             sg = RINGS[k][2]
             own = q_block(u, k, -sg * (2 + s))
-
             r1_s[rs, s, k] = r1_s[rs, s, k] + own[...]
         for k in range(COLORS):
             (st1(u, k, s + 1) if s < n - 2 else st2(u, k, 0)).start()
@@ -315,14 +304,10 @@
         return pl.ds(pl.multiple_of(r, RR), RR)
 
     def fetch(u):
-        return (pltpu.make_async_copy(xh_ref.at[shard_rows(u), :], fx_s, f_sem.at[0]),
-                pltpu.make_async_copy(dyh_ref.at[shard_rows(u), :], fd_s, f_sem.at[1]))
-
-    UE = early * PU
+        return (pltpu.make_async_copy(x_ref.at[shard_rows(u), :], fx_s, f_sem.at[0]),
+                pltpu.make_async_copy(dy_ref.at[shard_rows(u), :], fd_s, f_sem.at[1]))
+
     ag = Gather(me, gat_ref, fo_s, 0, PU, a_send, a_recv, ap_send, ap_recv, ao_sem)
-
-    def put(u):
-        return pltpu.make_async_copy(fo_s.at[UE + lax.rem(u, 2)], sh_ref.at[u - UE], fo_sem.at[lax.rem(u, 2)])
 
     def on_st2(u, s):
         for k in range(COLORS):
@@ -340,43 +325,22 @@
         if s == n - 2:
             for f in fetch(u):
                 f.wait()
-
             xhat, r = normalize(fx_s[...])
             total = jnp.concatenate([r2_s[rs, s, k] for k in range(COLORS)], axis=-1).astype(F32)
             dh = total * g_ref[...]
             gx = r * (dh - jnp.mean(dh, axis=-1, keepdims=True) - xhat * jnp.mean(dh * xhat, axis=-1, keepdims=True))
-            done = (fd_s[...].astype(F32) + gx).astype(BF)
-
-            @pl.when(u < UE)
-            def _():
-                fo_s[u] = done
-
-            @pl.when((u < UE) & (lax.rem(u, PU) == PU - 1))
+            fo_s[u] = (fd_s[...].astype(F32) + gx).astype(BF)
+
+            @pl.when(lax.rem(u, PU) == PU - 1)
             def _():
                 ag.begin(lax.div(u, PU))
 
-            @pl.when(u >= UE + 2)
-            def _():
-                put(u - 2).wait()
-
-            @pl.when(u >= UE)
-            def _():
-                fo_s[UE + lax.rem(u, 2)] = done
-                put(u).start()
-
-            @pl.when(u == nu - 1)
-            def _():
-                put(u - 1).wait()
-                put(u).wait()
-
     rs_at = (4, 10, 16, 22, 26, 30, 34)
-    ag_at = (6, 10, 14, 22, 30, 38)
-    steps = [on_st0] + [functools.partial(on_st1, s=s) for s in range(n - 1)] + [functools.partial(on_st2, s=s) for s in range(n - 1)]
-
-    def comm(r):
-        now = 4 * g + r
-        for rho, fn in reversed(list(zip(rs_at, steps, strict=True))):
-            if rho % 4 != r:
+    hops = [functools.partial(on_st1, s=s) for s in range(n - 1)] + [functools.partial(on_st2, s=s) for s in range(n - 1)]
+
+    def reduce_round(g, r, on_st0):
+        for rho, fn in reversed(list(zip(rs_at, [on_st0] + hops, strict=True))):
+            if rho % 4 != r or fn is None:
                 continue
             back = 3 + rho // 4
             u = lax.div(g - back, 2)
@@ -384,22 +348,24 @@
             @pl.when((g >= back) & (lax.rem(g - back + 2 * nt, 2) == 0) & (u < nu))
             def _():
                 fn(u)
-        for h, o in enumerate(ag_at):
-            first = 8 * (PU - 1) + 12 + rs_at[-1] + o
-            if first % 4 != r:
-                continue
-            p = lax.div(now - first, AG_EVERY)
-
-            @pl.when((now >= first) & (lax.rem(now - first + 64 * AG_EVERY, AG_EVERY) == 0) & (p < early))
-            def _():
-                ag.arrived(p, h)
-
-    def out_copy(sl, tt):
-        return pltpu.make_async_copy(ln_s.at[sl], lnh_ref.at[pl.ds(pl.multiple_of(tt * TM, TM), TM), :], ln_sem.at[sl])
-
-    @pl.when(g == 0)
-    def _():
+
+    def phase_one(wt_ref, wd_ref, wq_s, wu_s, x_s, dy_s, ln_s, h_s, da_s, qkv_s, do_s, dct_s, dc_o, og_o, st_s, dp_s, p_b, ds_b, p_s):
         WR = wq_s.shape[1]
+
+        def x_in(t):
+            return pltpu.make_async_copy(x_ref.at[tile_rows(t), :], x_s.at[lax.rem(t, 2)], x_sem.at[lax.rem(t, 2)])
+
+        def dy_in(t):
+            return pltpu.make_async_copy(dy_ref.at[tile_rows(t), :], dy_s.at[lax.rem(t, 2)], dy_sem.at[lax.rem(t, 2)])
+
+        def ln_out(t):
+            return pltpu.make_async_copy(ln_s.at[lax.rem(t, 2)], lnh_ref.at[tile_rows(t), :], ln_sem.at[lax.rem(t, 2)])
+
+        def dc_out(t):
+            return pltpu.make_async_copy(dc_o.at[lax.rem(t, 2)], dch_ref.at[:, tile_rows(t)], dc_sem.at[lax.rem(t, 2)])
+
+        def og_out(t):
+            return pltpu.make_async_copy(og_o.at[lax.rem(t, 2)], ogh_ref.at[:, tile_rows(t)], og_sem.at[lax.rem(t, 2)])
 
         def w_in(i):
             rows = pl.ds(pl.multiple_of(i * WR, WR), WR)
@@ -408,14 +374,14 @@
                     pltpu.make_async_copy(wuh_ref.at[rows, :], wu_s.at[j], wst_sem.at[j, 1]))
         whole = (pltpu.make_async_copy(woh_ref, wd_ref.at[pl.ds(0, d), :], w_sem.at[0]),
                  pltpu.make_async_copy(wdh_ref, wd_ref.at[pl.ds(d, F), :], w_sem.at[1]))
-        for cp in w_in(0) + w_in(1) + whole:
+        for cp in (x_in(0),) + w_in(0) + w_in(1) + (x_in(1),) + whole + (dy_in(0),):
             cp.start()
         me.greet()
-
         dct_s[...] = jnp.zeros_like(dct_s)
+        x_in(0).wait()
 
         def lnb(i, _):
-            ln_rows(x0_ref, ln_s.at[0], pl.ds(pl.multiple_of(i * 16, 16), 16), g_ref, b_ref)
+            ln_rows(x_s.at[0], ln_s.at[0], pl.ds(pl.multiple_of(i * 16, 16), 16), g_ref, b_ref)
             return 0
         lax.fori_loop(0, TM // 16, lnb, 0)
 
@@ -436,180 +402,207 @@
         for cp in whole:
             cp.wait()
 
-    live = g < nt
-
-    @pl.when((g > 0) & (g <= nt))
-    def _():
-        out_copy(nxt, g - 1).wait()
-
-    before = g + 3
-
-    def store(i, v):
-        p_s[lax.rem(lax.div(before, 2), 2), lax.rem(before, 2), :, :, :, pl.ds(i * NB, NB)] = v.reshape(n, n, RR, NB)
-    tile = Tile(ln_s.at[slot], dy_ref, wt_ref, wd_ref, dct_s, qkv_s, do_s, h_s, da_s,
-                og_ref, dc_ref, st_s, dp_s, p_b, ds_b, C, F, d, store)
-
-    comm(0)
-
-    @pl.when(live)
-    def _():
-        out_copy(slot, g).start()
-        tile.project(lambda i: ln_rows(x_ref, ln_s.at[nxt], pl.ds(i * 8, 8), g_ref, b_ref), TM // 8)
-
-    comm(2)
-
-    @pl.when(live)
-    def _():
-        tile.rest()
-
-    @pl.when(g == nt)
-    def _():
-        tile.last()
-
-    @pl.when((g > 0) & (g <= nt) & (slot == 0))
-    def _():
-        st0(lax.div(g, 2) - 1).start()
-
-    @pl.when(g == pl.num_programs(0) - 1)
-    def _():
-        ag.end(early)
-
-
-def forward(axis, side, x, dy, gain, bias, w_qkv, w_up, w_out, w_down, S, TM=256, PU=2, early=2):
+        def st0(u):
+            qi = lax.rem(u, QB)
+            return copy_to(p_s.at[lax.rem(u, 2), 1 - me.c], q_s.at[qi], s0_send.at[qi], s0_recv.at[qi], me.peer())
+
+        def on_st0(u):
+            st0(u).wait()
+            qi, pi = lax.rem(u, QB), lax.rem(u, 2)
+            for a in range(n):
+                for b in range(n):
+                    q_s[qi, a, b] = q_s[qi, a, b] + p_s[pi, me.c, a, b]
+            for k in range(COLORS):
+                st1(u, k, 0).start()
+
+        ag_at = (6, 10, 14, 22, 30, 38)
+
+        def comm(g, r):
+            reduce_round(g, r, on_st0)
+            now = 4 * g + r
+            for h, o in enumerate(ag_at):
+                first = 8 * (PU - 1) + 12 + rs_at[-1] + o
+                if first % 4 != r:
+                    continue
+                p = lax.div(now - first, AG_EVERY)
+
+                @pl.when((now >= first) & (lax.rem(now - first + 64 * AG_EVERY, AG_EVERY) == 0) & (p < early))
+                def _():
+                    ag.arrived(p, h)
+
+        def step(g, _):
+            slot = lax.rem(g, 2)
+            nxt = 1 - slot
+            live = g < nt
+            before = g + 3
+
+            def store(i, v):
+                p_s[lax.rem(lax.div(before, 2), 2), lax.rem(before, 2), :, :, :, pl.ds(i * NB, NB)] = v.reshape(n, n, RR, NB)
+            tile = Tile(ln_s.at[slot], dy_s.at[slot], wt_ref, wd_ref, dct_s, qkv_s, do_s, h_s, da_s,
+                        og_o.at[slot], dc_o.at[slot], st_s, dp_s, p_b, ds_b, C, F, d, store)
+
+            @pl.when((g > 0) & (g <= nt))
+            def _():
+                ln_out(g - 1).wait()
+
+            @pl.when((g > 1) & (g <= nt + 1))
+            def _():
+                dc_out(g - 2).wait()
+                og_out(g - 2).wait()
+
+            @pl.when(g + 2 < nt)
+            def _():
+                x_in(g + 2).start()
+
+            @pl.when(g + 1 < nt)
+            def _():
+                dy_in(g + 1).start()
+                x_in(g + 1).wait()
+
+            @pl.when(live)
+            def _():
+                dy_in(g).wait()
+                ln_out(g).start()
+
+            comm(g, 0)
+
+            @pl.when(live)
+            def _():
+                tile.project(lambda i: ln_rows(x_s.at[nxt], ln_s.at[nxt], pl.ds(i * 8, 8), g_ref, b_ref), TM // 8)
+
+            comm(g, 2)
+
+            @pl.when(live)
+            def _():
+                tile.rest()
+                dc_out(g).start()
+                og_out(g).start()
+
+            @pl.when(g == nt)
+            def _():
+                tile.last()
+
+            @pl.when((g > 0) & (g <= nt) & (slot == 0))
+            def _():
+                st0(lax.div(g, 2) - 1).start()
+            return 0
+        lax.fori_loop(0, first_steps, step, 0)
+
+    vm = pltpu.VMEM
+    WR = 512
+    pl.run_scoped(phase_one, vm((CF, D), BF), vm((dF, D), BF), vm((2, WR, C), BF), vm((2, WR, F), BF),
+                  vm((2, TM, D), BF), vm((2, TM, D), BF), vm((2, TM, D), BF), vm((F, TM), F32), vm((F, TM), F32),
+                  vm((C, TM), BF), vm((d, TM), BF), vm((TM, CF), BF), vm((2, CF, TM), BF), vm((2, dF, TM), BF),
+                  vm((S, S), F32), vm((S, S), F32), vm((S, S), BF), vm((S, S), BF),
+                  vm((2, CORES, side, side, RR, D), BF))
+
+    NC = 256
+    ng = D // NC
+    NP = nu // PU
+    gap = 5
+    at = (0, 1, 2, 5, 8, 11)
+    tail = max(0, -(-(gap * (NP - early - 1) + at[-1] + 1 - 2 * ng) // 2))
+
+    def phase_two(dc_s, og_s, lnb_s, dyb_s, o1_s, o2_s):
+        def block(i, which):
+            cs = pl.ds(pl.multiple_of(i * NC, NC), NC)
+            src, dst = ((lnh_ref, lnb_s), (dy_ref, dyb_s))[which]
+            return pltpu.make_async_copy(src.at[:, cs], dst, b_sem.at[which])
+
+        def out(i, which):
+            cs = pl.ds(pl.multiple_of(i * NC, NC), NC)
+            src, dst = ((o1_s, o1h_ref), (o2_s, o2h_ref))[which]
+            return pltpu.make_async_copy(src.at[lax.rem(i, 2)], dst.at[:, cs], o_sem.at[which, lax.rem(i, 2)])
+        left = (pltpu.make_async_copy(dch_ref, dc_s, l_sem.at[0]), pltpu.make_async_copy(ogh_ref, og_s, l_sem.at[1]))
+        left[0].start()
+        block(0, 0).start()
+        block(0, 1).start()
+        left[1].start()
+
+        def comm(g2, r):
+            reduce_round(g2 + first_steps, r, None)
+            half = 2 * g2 + r // 2
+            for h, o in enumerate(at):
+                p = lax.div(half - o, gap) + early
+
+                @pl.when((half >= o) & (lax.rem(half - o + 64 * gap, gap) == 0) & (p < NP))
+                def _():
+                    ag.arrived(p, h)
+
+        def step(g2, _):
+            live = g2 < ng
+            buf = lax.rem(g2, 2)
+
+            @pl.when(g2 == 0)
+            def _():
+                left[0].wait()
+
+            for j in range(2):
+                src, rhs, o_s, M = ((dc_s, lnb_s, o1_s, CF // 2), (og_s, dyb_s, o2_s, dF // 2))[j]
+                comm(g2, 2 * j)
+
+                @pl.when((g2 == 0) & (j == 1))
+                def _():
+                    left[1].wait()
+
+                @pl.when((g2 > 1) & live)
+                def _():
+                    out(g2 - 2, j).wait()
+
+                @pl.when(live)
+                def _():
+                    block(g2, j).wait()
+                    for i in range(2):
+                        rows = pl.ds(i * M, M)
+                        o_s[buf, rows, :] = jnp.dot(src[rows, :], rhs[...], preferred_element_type=F32).astype(BF)
+                    out(g2, j).start()
+
+                @pl.when(g2 + 1 < ng)
+                def _():
+                    block(g2 + 1, j).start()
+            return 0
+        lax.fori_loop(0, ng + tail, step, 0)
+        for j in range(2):
+            out(ng - 2, j).wait()
+            out(ng - 1, j).wait()
+        ag.end(NP)
+
+    pl.run_scoped(phase_two, vm((CF, T), BF), vm((dF, T), BF), vm((T, NC), BF), vm((T, NC), BF),
+                  vm((2, CF, NC), BF), vm((2, dF, NC), BF))
+
+
+def layer(axis, side, x, dy, gain, bias, w_qkv, w_up, w_out, w_down, S, TM=256, PU=2, early=2):
     T, D = x.shape
     C, F, d = w_qkv.shape[1], w_up.shape[1], w_out.shape[0]
     CF, dF = C + F, d + F
-    nt = T // TM
-    nu = nt // 2
+    nu = T // TM // 2
     RR = 2 * TM // (CORES * side * side)
-    drain = 10
     CW = D // COLORS
-    last = nt - 1
-    QB, RB, WR = 4, 5, 512
-    UE = early * PU
+    QB, RB = 4, 5
+    NP = nu // PU
     hops = 2 * (side - 1)
     dma = pltpu.SemaphoreType.DMA
     anyspace = pl.BlockSpec(memory_space=pl.ANY)
+    vm = pl.BlockSpec(memory_space=pltpu.VMEM)
     return pl.pallas_call(
-        functools.partial(forward_kernel, axis, side, S, d, C, F, nt, PU, early),
-        grid=(nt + drain,),
-        in_specs=[pl.BlockSpec((TM, D), lambda t: (0, 0), pipeline_mode=pl.Buffered(1)),
-                  pl.BlockSpec((TM, D), lambda t: (jnp.minimum(t + 1, last), 0)),
-                  pl.BlockSpec((TM, D), lambda t: (jnp.minimum(t, last), 0)),
-                  pl.BlockSpec((1, D), lambda t: (0, 0)),
-                  pl.BlockSpec((1, D), lambda t: (0, 0))] + [anyspace] * 6,
-        out_specs=[anyspace,
-                   pl.BlockSpec((CF, TM), lambda t: (0, jnp.minimum(t, last))),
-                   pl.BlockSpec((dF, TM), lambda t: (0, jnp.minimum(t, last))),
-                   anyspace, anyspace],
-        out_shape=[jax.ShapeDtypeStruct((T, D), BF), jax.ShapeDtypeStruct((CF, T), BF),
-                   jax.ShapeDtypeStruct((dF, T), BF), jax.ShapeDtypeStruct((nu - UE, RR, D), BF),
-                   jax.ShapeDtypeStruct((nu, CORES, side, side, RR, D), BF)],
-        scratch_shapes=[pltpu.VMEM((CF, D), BF), pltpu.VMEM((dF, D), BF),
-                        pltpu.VMEM((2, WR, C), BF), pltpu.VMEM((2, WR, F), BF),
-                        pltpu.VMEM((2, TM, D), BF), pltpu.VMEM((F, TM), F32), pltpu.VMEM((F, TM), F32),
-                        pltpu.VMEM((C, TM), BF), pltpu.VMEM((d, TM), BF), pltpu.VMEM((TM, CF), BF),
-                        pltpu.VMEM((S, S), F32), pltpu.VMEM((S, S), F32), pltpu.VMEM((S, S), BF), pltpu.VMEM((S, S), BF),
-                        pltpu.VMEM((2, CORES, side, side, RR, D), BF),
-                        pltpu.VMEM((QB, side, side, RR, D), BF),
+        functools.partial(layer_kernel, axis, side, S, TM, C, F, d, PU, early),
+        in_specs=[anyspace, anyspace, vm, vm] + [anyspace] * 4,
+        out_specs=[anyspace] * 6,
+        out_shape=[jax.ShapeDtypeStruct((T, D), BF), jax.ShapeDtypeStruct((CF, T), BF), jax.ShapeDtypeStruct((dF, T), BF),
+                   jax.ShapeDtypeStruct((nu, CORES, side, side, RR, D), BF),
+                   jax.ShapeDtypeStruct((CF, D), BF), jax.ShapeDtypeStruct((dF, D), BF)],
+        scratch_shapes=[pltpu.VMEM((QB, side, side, RR, D), BF),
                         pltpu.VMEM((RB, side - 1, COLORS, side, RR, CW), BF),
                         pltpu.VMEM((RB, side - 1, COLORS, RR, CW), BF),
-                        pltpu.VMEM((RR, D), BF), pltpu.VMEM((RR, D), BF), pltpu.VMEM((UE + 2, RR, D), BF),
-                        dma((2,)), dma((2, 2)), dma((2,)), dma((QB,)), dma((QB,)),
+                        pltpu.VMEM((RR, D), BF), pltpu.VMEM((RR, D), BF), pltpu.VMEM((nu, RR, D), BF),
+                        dma((2,)), dma((2, 2)), dma((2,)), dma((2,)), dma((2,)), dma((2,)), dma((2,)), dma((QB,)), dma((QB,)),
                         dma((RB, side - 1, COLORS)), dma((RB, side - 1, COLORS)),
                         dma((RB, side - 1, COLORS)), dma((RB, side - 1, COLORS)),
-                        dma((2,)), dma((2,)),
-                        dma((early, COLORS, hops)), dma((early, COLORS, hops)), dma, dma, dma((early,))],
+                        dma((2,)), dma((NP, COLORS, hops)), dma((NP, COLORS, hops)), dma, dma, dma((NP,)),
+                        dma((2,)), dma((2,)), dma((2, 2))],
         compiler_params=pltpu.CompilerParams(vmem_limit_bytes=VMEM_LIMIT, collective_id=1, has_side_effects=True),
-        name="forward_rs",
-    )(x, x, dy, gain.reshape(1, D), bias.reshape(1, D), w_qkv, w_up, w_out, w_down, x, dy)
-
-
-def gather_kernel(axis, side, base, PU, sh_ref, dc_ref, og_ref, ln_ref, dy_ref, gin_ref, o1_ref, o2_ref, g_ref,
-                  own_s, dc_s, og_s, l_sem, dc_sem, og_sem, snd, rcv, p_snd, p_rcv, own_sem):
-    me = Place(axis, side)
-    g = pl.program_id(0)
-    ng = pl.num_programs(0)
-    nl = sh_ref.shape[0]
-    NP = nl // PU
-    HA = side - 1
-    M1, M2 = dc_s.shape[0] // 2, og_s.shape[0] // 2
-    ag = Gather(me, g_ref, own_s, base, PU, snd, rcv, p_snd, p_rcv, own_sem)
-
-    def left(j):
-        src, dst, sem, M = ((dc_ref, dc_s, dc_sem, M1), (og_ref, og_s, og_sem, M2))[j // 2]
-        rows = pl.ds((j % 2) * M, M)
-        return pltpu.make_async_copy(src.at[rows, :], dst.at[rows, :], sem.at[j % 2])
-
-    @pl.when(g == 0)
-    def _():
-        ld = pltpu.make_async_copy(sh_ref, own_s, l_sem)
-        ld.start()
-        left(0).start()
-        me.greet()
-        ld.wait()
-        for p in range(NP):
-            ag.begin(p)
-        left(1).start()
-        left(2).start()
-        left(3).start()
-
-    for j in range(2):
-        @pl.when(g == 0)
-        def _():
-            left(2 * j).wait()
-            left(2 * j + 1).wait()
-        src, rhs, o_ref, M = ((dc_s, ln_ref, o1_ref, M1), (og_s, dy_ref, o2_ref, M2))[j]
-        for i in range(2):
-            rows = pl.ds(i * M, M)
-            o_ref[rows, :] = jnp.dot(src[rows, :], rhs[...], preferred_element_type=F32).astype(BF)
-        now = 2 * g + j
-        half = -(-NP // 2)
-        for h in range(HA):
-            for i in range(half):
-                p = lax.rem(now, 2) * half + i
-
-                @pl.when((lax.div(now, 2) == h) & (p < NP))
-                def _():
-                    ag.arrived(p, h)
-        left_rounds = 2 * ng - 2 * HA - 1
-        many = HA * NP
-        e = (now - 2 * HA - 1) * many
-        for h in range(HA, 2 * HA):
-            p = lax.div(e, left_rounds) - (h - HA) * NP
-
-            @pl.when((e >= 0) & (lax.rem(e, left_rounds) < many) & (p >= 0) & (p < NP))
-            def _():
-                ag.arrived(p, h)
-
-    @pl.when(g == ng - 1)
-    def _():
-        ag.end(NP)
-
-
-def gather(axis, side, sh, dc, og, ln, dy, gathered, PU=2, NB=256):
-    nl, RR, D = sh.shape
-    nu = gathered.shape[0]
-    CF, T = dc.shape
-    dF = og.shape[0]
-    NP = nl // PU
-    hops = 2 * (side - 1)
-    dma = pltpu.SemaphoreType.DMA
-    anyspace = pl.BlockSpec(memory_space=pl.ANY)
-    return pl.pallas_call(
-        functools.partial(gather_kernel, axis, side, nu - nl, PU),
-        grid=(D // NB,),
-        in_specs=[anyspace] * 3 + [pl.BlockSpec((T, NB), lambda t: (0, t))] * 2 + [anyspace],
-        out_specs=[pl.BlockSpec((CF, NB), lambda t: (0, t)), pl.BlockSpec((dF, NB), lambda t: (0, t)), anyspace],
-        out_shape=[jax.ShapeDtypeStruct((CF, D), BF), jax.ShapeDtypeStruct((dF, D), BF),
-                   jax.ShapeDtypeStruct(gathered.shape, BF)],
-        scratch_shapes=[pltpu.VMEM((nl, RR, D), BF), pltpu.VMEM((CF, T), BF), pltpu.VMEM((dF, T), BF),
-                        dma, dma((2,)), dma((2,)),
-                        dma((NP, COLORS, hops)), dma((NP, COLORS, hops)), dma, dma, dma((NP,))],
-        input_output_aliases={5: 2},
-        compiler_params=pltpu.CompilerParams(vmem_limit_bytes=VMEM_LIMIT, collective_id=2, has_side_effects=True),
-        name="gather_grads",
-    )(sh, dc, og, ln, dy, gathered)
+        name="layer_grads",
+    )(x, dy, gain.reshape(1, D), bias.reshape(1, D), w_qkv, w_up, w_out, w_down)
 
 
 def finish_kernel(d, C, o1_ref, o2_ref, gh_ref, gw_ref, gd_ref, gq_ref, gu_ref, dx_ref, buf, isem, osem):
@@ -688,8 +681,7 @@
         d = w_out.shape[0]
         x = tokens.reshape(T, D)
         dy = grad_out.reshape(T, D)
-        ln, dc, og, sh, gathered = forward('tp', side, x, dy, ln_gain, ln_bias, w_qkv.reshape(D, C), w_up, w_out, w_down, seq)
-        o1, o2, gathered = gather('tp', side, sh, dc, og, ln, dy, gathered)
+        _, _, _, gathered, o1, o2 = layer('tp', side, x, dy, ln_gain, ln_bias, w_qkv.reshape(D, C), w_up, w_out, w_down, seq)
         gw, gd, gq, gu, dx = finish(d, C, o1, o2, gathered.reshape(T, D))
         return dx.reshape(tokens.shape), gq.reshape(w_qkv.shape), gw, gu, gd
 

time: 520 us -> 498 us (0.958)
  Pallas kernels: 519 us -> 497 us
    pallas_call x2 -> x1, Pallas kernels: 467 us -> 445 us  [layer(): pl.pallas_call(functools.partial(layer_kernel, axis, side, S, TM, C, F, d...]
where the time goes in v3:
time: 498 us
  Pallas kernels  497 us (100%)
    pallas_call x1, Pallas kernels, layer(): pl.pallas_call(functools.partial(layer_kernel, axis, side, S, TM, C, F, d...  445 us
    pallas_call x1, Pallas kernels, finish(): pl.pallas_call(functools.partial(finish_kernel, d, C), grid=(steps,), in_...  52.1 us

profile of v3, /device:TPU:97, one launch (start us, length us, event | category | flops | bytes accessed | tf_op | source)
XLA Modules:
  0.0 498.1 jit_solution(6841912729661288671)
XLA Ops:
  0.6 445.2 %layer_grads.1 = (bf16[8192,4096]{1,0:T(8,128)(2,1)}, bf16[896,8192]{1,0:T(8,128)(2,1)}, bf16[640,8192]{1,0:T(8,128)(2,1)}, bf16[16,2,4,4,16,4096]{5,4,3,2,1,0:T...) custom-call(bf16[8192,4096]{1,0:T(8,128)(2,1)} %bitcast.x_ref, bf16[8192,4096]{1,0:T(8,128)(2,1)} %bitcast.1.dy_ref, ...), custom_call_target="tpu_custom_call" | custom-call | tf_op jit(solution)/shard_map/layer_grads/pallas_call | solution.py:587
  445.9 52.1 %finish_grads.1 = (bf16[128,4096]{1,0:T(8,128)(2,1)}, bf16[512,4096]{1,0:T(8,128)(2,1)}, bf16[4096,384]{1,0:T(8,128)(2,1)}, bf16[4096,512]{1,0:T(8,128)(2,1)}, bf16[8192,4096]{1,0:T(8,128)(2,1)}) custom-call(bf16[896,4096]{1,0:T(8,128)(2,1)} %get-tuple-element.13.o1_ref, bf16[640,4096]{1,0:T(8,128)(2,1)} %get-tuple-element.14.o2_ref, ...), custom_call_target="tpu_custom_call" | custom-call | tf_op jit(solution)/shard_map/finish_grads/pallas_call | solution.py:651
